TPU v7x, 32 devices: a whole 2x2x4 slice. The times are simulated.
32 devices in a mesh: dp: 2 (over x), tp: 4 (over z), cp: 4 (over y, core).
Axes of the slice: x: 2, y: 2, z: 4, core: 2. Of those that a mesh axis runs over, the one named last changes fastest.
Arguments:
- hidden: bfloat16 [8192, 3840], P(('dp', 'cp')), parts along dimension 0
- start_pos: int32 [2], P('dp'), parts along dimension 0
- k_local: bfloat16 [2048, 8, 256], P('dp', 'tp'), parts along dimension 0
- v_local: bfloat16 [2048, 8, 256], P('dp', 'tp'), parts along dimension 0
- k_global: bfloat16 [49152, 8, 256], P(('dp', 'cp'), 'tp'), parts along dimension 0
- v_global: bfloat16 [49152, 8, 256], P(('dp', 'cp'), 'tp'), parts along dimension 0
- w_query: bfloat16 [2, 3840, 4096], P(None, None, 'tp')
- w_key: bfloat16 [2, 3840, 2048], P(None, None, 'tp')
- w_value: bfloat16 [2, 3840, 2048], P(None, None, 'tp')
- w_out: bfloat16 [2, 4096, 3840], P(None, 'tp')
- w_gate: bfloat16 [2, 3840, 15360], P(None, None, 'tp')
- w_up: bfloat16 [2, 3840, 15360], P(None, None, 'tp')
- w_down: bfloat16 [2, 15360, 3840], P(None, 'tp')
- norm_gain: float32 [2, 4, 3840], replicated
- qk_gain: float32 [2, 2, 256], replicated
Outputs:
- output 1: bfloat16 [8192, 3840], P(('dp', 'cp')), parts along dimension 0
- output 2: bfloat16 [8192, 8, 256], P(('dp', 'cp'), 'tp'), parts along dimension 0
- output 3: bfloat16 [8192, 8, 256], P(('dp', 'cp'), 'tp'), parts along dimension 0
- output 4: bfloat16 [8192, 8, 256], P(('dp', 'cp'), 'tp'), parts along dimension 0
- output 5: bfloat16 [8192, 8, 256], P(('dp', 'cp'), 'tp'), parts along dimension 0
There are 2 independent parts. A program takes and returns all parts, laid end to end along the dimension named above; an argument that names none is the same for every part.
All inputs are finite; a program needn't handle non-finite values.
Results may differ from a plain program's by a relative error of at most 0.02.
Values are sent between devices in bfloat16 or wider.
A program may use at most 1 GiB of HBM per device.

v0:
```python
import jax
import jax.numpy as jnp
from jax import lax
from jax.sharding import PartitionSpec as P

NORM_EPS = 1e-6
LOCAL_BASE = 10000.0
GLOBAL_BASE = 1000000.0
GLOBAL_DIV = 8.0
NEG_BIG = -1e30


def rms_scale(values, gain_vec):
    return values * lax.rsqrt(jnp.mean(values * values, axis=-1, keepdims=True) + NORM_EPS) * (1.0 + gain_vec)


def rotate(values, positions, rope_base, divisor):
    half_dim = values.shape[-1] // 2
    inv_freq = 1.0 / (rope_base ** (jnp.arange(0, 2 * half_dim, 2, dtype=jnp.float32) / (2 * half_dim)))
    angles = (positions.astype(jnp.float32) / divisor)[:, None] * inv_freq[None, :]
    angles = jnp.concatenate([angles, angles], axis=-1)[:, None, :]
    turned = jnp.concatenate([-values[..., half_dim:], values[..., :half_dim]], axis=-1)
    return values * jnp.cos(angles) + turned * jnp.sin(angles)


def project(hidden, layer_gains, qk_pair, w_query, w_key, w_value, positions, rope_base, divisor):
    row_count = hidden.shape[0]
    head_dim = qk_pair.shape[-1]
    normed = rms_scale(hidden.astype(jnp.float32), layer_gains[0]).astype(jnp.bfloat16)
    queries = jnp.dot(normed, w_query, preferred_element_type=jnp.float32).reshape(row_count, -1, head_dim)
    key_new = jnp.dot(normed, w_key, preferred_element_type=jnp.float32).reshape(row_count, -1, head_dim)
    value_new = jnp.dot(normed, w_value, preferred_element_type=jnp.float32).astype(jnp.bfloat16).reshape(row_count, -1, head_dim)
    queries = rotate(rms_scale(queries, qk_pair[0]), positions, rope_base, divisor).astype(jnp.bfloat16)
    key_new = rotate(rms_scale(key_new, qk_pair[1]), positions, rope_base, divisor).astype(jnp.bfloat16)
    return queries.reshape(row_count, key_new.shape[1], -1, head_dim), key_new, value_new


def finish(hidden, attn_out, layer_gains, w_out, w_gate, w_up, w_down):
    row_count = hidden.shape[0]
    attn_proj = lax.psum(jnp.dot(attn_out.reshape(row_count, -1), w_out, preferred_element_type=jnp.float32).astype(jnp.bfloat16), 'tp')
    residual = (hidden.astype(jnp.float32) + rms_scale(attn_proj.astype(jnp.float32), layer_gains[1])).astype(jnp.bfloat16)
    normed = rms_scale(residual.astype(jnp.float32), layer_gains[2]).astype(jnp.bfloat16)
    gate_proj = jnp.dot(normed, w_gate, preferred_element_type=jnp.float32)
    up_proj = jnp.dot(normed, w_up, preferred_element_type=jnp.float32)
    hidden_act = (jax.nn.gelu(gate_proj, approximate=True) * up_proj).astype(jnp.bfloat16)
    down_proj = lax.psum(jnp.dot(hidden_act, w_down, preferred_element_type=jnp.float32).astype(jnp.bfloat16), 'tp')
    return (residual.astype(jnp.float32) + rms_scale(down_proj.astype(jnp.float32), layer_gains[3])).astype(jnp.bfloat16)


def window_attention(queries, key_new, value_new, k_cache, v_cache, first_pos, positions, cp_index, cp_size):
    row_count = queries.shape[0]
    window = k_cache.shape[0]
    tail_len = min(window, row_count)
    step_count = min(cp_size - 1, -(-window // row_count))
    key_parts = [k_cache]
    value_parts = [v_cache]
    pos_parts = [first_pos - window + jnp.remainder(jnp.arange(window) - first_pos, window)]
    ok_parts = [jnp.ones((window,), dtype=bool)]
    for step_back in range(step_count, 0, -1):
        sender_pairs = [(sender, sender + step_back) for sender in range(cp_size - step_back)]
        got_key, got_value = lax.ppermute((key_new[row_count - tail_len:], value_new[row_count - tail_len:]), 'cp', sender_pairs)
        key_parts.append(got_key)
        value_parts.append(got_value)
        pos_parts.append(positions[row_count - tail_len:] - step_back * row_count)
        ok_parts.append(jnp.broadcast_to(cp_index >= step_back, (tail_len,)))
    key_parts.append(key_new)
    value_parts.append(value_new)
    pos_parts.append(positions)
    ok_parts.append(jnp.ones((row_count,), dtype=bool))
    key_all = jnp.concatenate(key_parts, axis=0)
    value_all = jnp.concatenate(value_parts, axis=0)
    key_pos = jnp.concatenate(pos_parts)
    key_ok = jnp.concatenate(ok_parts)
    distance = positions[:, None] - key_pos[None, :]
    visible = key_ok[None, :] & (distance >= 0) & (distance < window)
    scores = jnp.einsum('qkgd,tkd->qkgt', queries, key_all, preferred_element_type=jnp.float32) * queries.shape[-1] ** -0.5
    scores = jnp.where(visible[:, None, None, :], scores, NEG_BIG)
    attn_prob = jax.nn.softmax(scores, axis=-1).astype(jnp.bfloat16)
    return jnp.einsum('qkgt,tkd->qkgd', attn_prob, value_all, preferred_element_type=jnp.float32).astype(jnp.bfloat16)


def partial_block(block_q, query_rel, cache_k, cache_v, cache_ok, own_k, own_v, own_rel):
    scale = block_q.shape[-1] ** -0.5
    cache_scores = jnp.einsum('qkgd,tkd->qkgt', block_q, cache_k, preferred_element_type=jnp.float32) * scale
    cache_scores = jnp.where(cache_ok[None, None, None, :], cache_scores, NEG_BIG)
    own_scores = jnp.einsum('qkgd,tkd->qkgt', block_q, own_k, preferred_element_type=jnp.float32) * scale
    own_seen = own_rel[None, :] <= query_rel[:, None]
    own_scores = jnp.where(own_seen[:, None, None, :], own_scores, NEG_BIG)
    row_max = jnp.maximum(cache_scores.max(axis=-1), own_scores.max(axis=-1))
    cache_exp = jnp.exp(cache_scores - row_max[..., None])
    own_exp = jnp.exp(own_scores - row_max[..., None])
    row_sum = cache_exp.sum(axis=-1) + own_exp.sum(axis=-1)
    weighted = jnp.einsum('qkgt,tkd->qkgd', cache_exp.astype(jnp.bfloat16), cache_v, preferred_element_type=jnp.float32)
    weighted = weighted + jnp.einsum('qkgt,tkd->qkgd', own_exp.astype(jnp.bfloat16), own_v, preferred_element_type=jnp.float32)
    return weighted, jnp.stack([row_max, row_sum], axis=-1)


def merge_parts(part_out, part_stats):
    best_max = part_stats[..., 0].max(axis=0)
    factors = jnp.exp(part_stats[..., 0] - best_max)
    norm_sum = (factors * part_stats[..., 1]).sum(axis=0)
    weighted = (part_out * factors[..., None]).sum(axis=0)
    return (weighted / norm_sum[..., None]).astype(jnp.bfloat16)


def spread_attention(queries, key_new, value_new, k_cache, v_cache, first_pos, cp_index, cp_size):
    row_count = queries.shape[0]
    shard_len = k_cache.shape[0]
    all_queries = lax.all_gather(queries, 'cp')
    cache_ok = (cp_index * shard_len + jnp.arange(shard_len)) < first_pos
    own_rel = cp_index * row_count + jnp.arange(row_count)

    def one_block(block_args):
        block_q, block_index = block_args
        query_rel = block_index * row_count + jnp.arange(row_count)
        return partial_block(block_q, query_rel, k_cache, v_cache, cache_ok, key_new, value_new, own_rel)

    part_out, part_stats = lax.map(one_block, (all_queries, jnp.arange(cp_size)))
    got_out = lax.all_to_all(part_out, 'cp', 0, 0, tiled=True)
    got_stats = lax.all_to_all(part_stats, 'cp', 0, 0, tiled=True)
    return merge_parts(got_out, got_stats)


def solution(mesh):
    cp_size = mesh.shape['cp']
    row_spec = P(('dp', 'cp'), None)
    cache_spec = P(('dp', 'cp'), 'tp', None)
    window_spec = P('dp', 'tp', None)
    col_spec = P(None, None, 'tp')
    row_split = P(None, 'tp', None)
    replicated = P()

    def device_step(hidden, start_pos, k_local, v_local, k_global, v_global, w_query, w_key, w_value, w_out, w_gate, w_up, w_down, norm_gain, qk_gain):
        first_pos = start_pos[0]
        cp_index = lax.axis_index('cp')
        row_count = hidden.shape[0]
        positions = first_pos + cp_index * row_count + jnp.arange(row_count)
        queries, key_loc, value_loc = project(hidden, norm_gain[0], qk_gain[0], w_query[0], w_key[0], w_value[0], positions, LOCAL_BASE, 1.0)
        attn_out = window_attention(queries, key_loc, value_loc, k_local, v_local, first_pos, positions, cp_index, cp_size)
        middle = finish(hidden, attn_out, norm_gain[0], w_out[0], w_gate[0], w_up[0], w_down[0])
        queries, key_glob, value_glob = project(middle, norm_gain[1], qk_gain[1], w_query[1], w_key[1], w_value[1], positions, GLOBAL_BASE, GLOBAL_DIV)
        attn_out = spread_attention(queries, key_glob, value_glob, k_global, v_global, first_pos, cp_index, cp_size)
        final_out = finish(middle, attn_out, norm_gain[1], w_out[1], w_gate[1], w_up[1], w_down[1])
        return final_out, key_loc, value_loc, key_glob, value_glob

    return jax.shard_map(device_step, mesh=mesh, in_specs=(row_spec, P('dp'), window_spec, window_spec, cache_spec, cache_spec, col_spec, col_spec, col_spec, row_split, col_spec, col_spec, row_split, replicated, replicated), out_specs=(row_spec, cache_spec, cache_spec, cache_spec, cache_spec), check_vma=False)
```

profile of v0, /device:TPU:4, one launch (start us, length us, event | category | flops | bytes accessed | tf_op | source)
XLA Modules:
  0.0 2420.1 jit_solution(7116681162723985910)
XLA Ops:
  24.4 8.3 multiply_reduce_fusion.4
  46.1 10.5 fusion.164
  64.8 10.6 copy.64
  75.4 13.2 multiply_reduce_fusion.2
  110.6 27.8 %fusion.204 = (f32[1024,2,2]{0,2,1:T(2,128)S(1)}, f32[1024,2,2,3072]{0,3,2,1:T(8,128)}) fusion(pred[1024,3072]{0,1:T(8,128)(4,1)S(1)} %fusion.107, bf16[1024,2,2,256]{0,3,2,1:T(8,128)(2,1)} %bitcast.279, bf16[1024,2,256]{0,2,1:T(8,128)(2,1)} %fusion.159, bf16[1024,2,256]{0,2,1:T(8,128)(2,1)} %collective-permute-done.1, bf16[1024,2,256]{0,2,1:T(8,128)(2,1)} %copy.63), kind=kOutput, calls=%fused_computation.268 | convolution fusion | flops 6502222848 | bytes 58736640 | tf_op jit(solution)/shard_map/sub | solution.py:78
  138.5 19.4 fusion.162
  157.8 13.9 fusion.126
  171.9 274.7 %all-reduce.5.cloned.1.call-done = bf16[1024,3840]{1,0:T(8,128)(2,1)} async-done(((bf16[1024,3840]{1,0:T(8,128)(2,1)}), bf16[1024,3840]{1,0:T(8,128)(2,1)}) %all-reduce.5.cloned.1.call-update) | async-done | bytes 7864336 | tf_op jit(solution)/shard_map/psum | solution.py:40
  459.1 39.4 %fusion.52 = f32[1024,3840]{1,0:T(8,128)} fusion(bf16[2,3840,3840]{2,1,0:T(8,128)(2,1)} %param.27, bf16[1024,3840]{1,0:T(8,128)(2,1)S(1)} %get-tuple-element.183, f32[3840]{0:T(1024)S(1)} %copy-done.23, f32[1024]{0:T(1024)S(1)} %add_rsqrt_fusion.9), kind=kOutput, calls=%fused_computation.60 | convolution fusion | flops 30214717440 | bytes 53103616 | tf_op jit(solution)/shard_map/dot_general | solution.py:43
  498.4 39.2 %fusion.88 = bf16[1024,3840]{1,0:T(8,128)(2,1)} fusion(f32[1024,3840]{1,0:T(8,128)} %fusion.52, bf16[2,3840,3840]{2,1,0:T(8,128)(2,1)} %param.28, bf16[1024,3840]{1,0:T(8,128)(2,1)S(1)} %get-tuple-element.183, f32[3840]{0:T(1024)S(1)} %copy-done.23, f32[1024]{0:T(1024)S(1)} %add_rsqrt_fusion.9), kind=kOutput, calls=%fused_computation.121 | convolution fusion | flops 30254039040 | bytes 60967936 | tf_op jit(solution)/shard_map/dot_general | solution.py:44
  537.7 37.7 %fusion.132 = bf16[1024,3840]{1,0:T(8,128)(2,1)} fusion(bf16[1024,3840]{1,0:T(8,128)(2,1)} %fusion.88, bf16[2,3840,3840]{2,1,0:T(8,128)(2,1)} %param.29), kind=kOutput, calls=%fused_computation.159 | convolution fusion | flops 30202920960 | bytes 45219840 | tf_op jit(solution)/shard_map/dot_general | solution.py:46
  575.5 10.6 copy.68
  589.9 257.3 %all-reduce.7.cloned.1.call-done = bf16[1024,3840]{1,0:T(8,128)(2,1)} async-done(((bf16[1024,3840]{1,0:T(8,128)(2,1)}), bf16[1024,3840]{1,0:T(8,128)(2,1)}) %all-reduce.7.cloned.1.call-update) | async-done | bytes 7864336 | tf_op jit(solution)/shard_map/psum | solution.py:46
  860.3 8.5 multiply_reduce_fusion.1
  895.8 8.7 fusion.167
  905.9 8.2 multiply_reduce_fusion.3
  916.8 16.4 all-gather.2.cloned.1.call-done
  933.2 569.1 %while.13 = (s32[]{:T(128)}, f32[4,1024,2,2,256]{4,1,3,2,0:T(8,128)}, f32[4,1024,2,2,2]{1,3,2,4,0:T(2,128)S(1)}, bf16[4,1024,2,2,256]{4,1,3,2,0:T(8,128)(2,1)}, ...) while((s32[]{:T(128)}, ...), condition=%wide.region_18.19_spmd.clone, body=%wide.region_13.18_spmd.clone.sunk | while | flops 30389843968 | bytes 392505024 | solution.py:118
  935.4 10.5 bitcast_reduce_fusion.5
  946.6 38.0 %bitcast_reduce_fusion.6 = (f32[1024,2,2]{0,2,1:T(2,128)S(1)}, f32[2,1024,2,6144]{3,1,2,0:T(8,128)}) fusion(pred[6144]{0:T(1024)(128)(4,1)S(1)} %add_compare_fusion.2, bf16[6144,2,256]{2,0,1:T(8,128)(2,1)} %get-tuple-element.339, bf16[4,1024,2,2,256]{4,1,3,2,0:T(8,128)(2,1)} %get-tuple-element.338, s32[]{:T(128)} %get-tuple-element.321), kind=kOutput, calls=%fused_computation.3.clone.1 | convolution fusion | flops 12960395264 | bytes 109074944 | tf_op jit(solution)/shard_map/while/body/eval_jaxpr/qkgd,tkd->qkgt/dot_general | solution.py:84
  984.6 31.3 %fusion.228 = f32[1024,2,2]{0,2,1:T(2,128)S(1)} fusion(f32[2,1024,2,6144]{3,1,2,0:T(8,128)} %get-tuple-element.306, f32[1024,2,2]{0,2,1:T(2,128)S(1)} %max.19, pred[6144]{0:T(1024)(128)(4,1)S(1)} %add_compare_fusion.2), kind=kLoop, calls=%fused_computation.6.clone.1 | loop fusion | flops 100659200 | bytes 100702208 | tf_op jit(solution)/shard_map/while/body/eval_jaxpr/reduce_sum | solution.py:92
  1015.9 7.8 fusion.229
  1023.8 13.2 fusion.227
  1037.0 38.8 %bitcast_dynamic-update-slice_fusion.2 = f32[4,1024,2,2,256]{4,1,3,2,0:T(8,128)} fusion(f32[4,1024,2,2,256]{4,1,3,2,0:T(8,128)} %get-tuple-element.322, s32[]{:T(128)} %get-tuple-element.321, f32[2,1024,2,256]{3,1,2,0:T(8,128)} %fusion.227, bf16[6144,2,256]{2,0,1:T(8,128)(2,1)} %get-tuple-element.342, f32[2,1024,2,6144]{3,1,2,0:T(8,128)} %get-tuple-element.306, ...), kind=kOutput, calls=%fused_computation.24.clone.1 | convolution fusion | flops 12986613760 | bytes 115366400 | tf_op jit(solution)/shard_map/while/body/eval_jaxpr/qkgt,tkd->qkgd/dot_general | solution.py:93
  1077.6 10.5 bitcast_reduce_fusion.5
  1088.7 38.0 %bitcast_reduce_fusion.6 = (f32[1024,2,2]{0,2,1:T(2,128)S(1)}, f32[2,1024,2,6144]{3,1,2,0:T(8,128)}) fusion(pred[6144]{0:T(1024)(128)(4,1)S(1)} %add_compare_fusion.2, bf16[6144,2,256]{2,0,1:T(8,128)(2,1)} %get-tuple-element.339, bf16[4,1024,2,2,256]{4,1,3,2,0:T(8,128)(2,1)} %get-tuple-element.338, s32[]{:T(128)} %get-tuple-element.321), kind=kOutput, calls=%fused_computation.3.clone.1 | convolution fusion | flops 12960395264 | bytes 109074944 | tf_op jit(solution)/shard_map/while/body/eval_jaxpr/qkgd,tkd->qkgt/dot_general | solution.py:84
  1126.8 31.3 %fusion.228 = f32[1024,2,2]{0,2,1:T(2,128)S(1)} fusion(f32[2,1024,2,6144]{3,1,2,0:T(8,128)} %get-tuple-element.306, f32[1024,2,2]{0,2,1:T(2,128)S(1)} %max.19, pred[6144]{0:T(1024)(128)(4,1)S(1)} %add_compare_fusion.2), kind=kLoop, calls=%fused_computation.6.clone.1 | loop fusion | flops 100659200 | bytes 100702208 | tf_op jit(solution)/shard_map/while/body/eval_jaxpr/reduce_sum | solution.py:92
  1165.9 13.2 fusion.227
  1179.1 38.8 %bitcast_dynamic-update-slice_fusion.2 = f32[4,1024,2,2,256]{4,1,3,2,0:T(8,128)} fusion(f32[4,1024,2,2,256]{4,1,3,2,0:T(8,128)} %get-tuple-element.322, s32[]{:T(128)} %get-tuple-element.321, f32[2,1024,2,256]{3,1,2,0:T(8,128)} %fusion.227, bf16[6144,2,256]{2,0,1:T(8,128)(2,1)} %get-tuple-element.342, f32[2,1024,2,6144]{3,1,2,0:T(8,128)} %get-tuple-element.306, ...), kind=kOutput, calls=%fused_computation.24.clone.1 | convolution fusion | flops 12986613760 | bytes 115366400 | tf_op jit(solution)/shard_map/while/body/eval_jaxpr/qkgt,tkd->qkgd/dot_general | solution.py:93
  1219.7 10.5 bitcast_reduce_fusion.5
  1230.9 38.0 %bitcast_reduce_fusion.6 = (f32[1024,2,2]{0,2,1:T(2,128)S(1)}, f32[2,1024,2,6144]{3,1,2,0:T(8,128)}) fusion(pred[6144]{0:T(1024)(128)(4,1)S(1)} %add_compare_fusion.2, bf16[6144,2,256]{2,0,1:T(8,128)(2,1)} %get-tuple-element.339, bf16[4,1024,2,2,256]{4,1,3,2,0:T(8,128)(2,1)} %get-tuple-element.338, s32[]{:T(128)} %get-tuple-element.321), kind=kOutput, calls=%fused_computation.3.clone.1 | convolution fusion | flops 12960395264 | bytes 109074944 | tf_op jit(solution)/shard_map/while/body/eval_jaxpr/qkgd,tkd->qkgt/dot_general | solution.py:84
  1268.9 31.3 %fusion.228 = f32[1024,2,2]{0,2,1:T(2,128)S(1)} fusion(f32[2,1024,2,6144]{3,1,2,0:T(8,128)} %get-tuple-element.306, f32[1024,2,2]{0,2,1:T(2,128)S(1)} %max.19, pred[6144]{0:T(1024)(128)(4,1)S(1)} %add_compare_fusion.2), kind=kLoop, calls=%fused_computation.6.clone.1 | loop fusion | flops 100659200 | bytes 100702208 | tf_op jit(solution)/shard_map/while/body/eval_jaxpr/reduce_sum | solution.py:92
  1308.1 13.2 fusion.227
  1321.2 38.8 %bitcast_dynamic-update-slice_fusion.2 = f32[4,1024,2,2,256]{4,1,3,2,0:T(8,128)} fusion(f32[4,1024,2,2,256]{4,1,3,2,0:T(8,128)} %get-tuple-element.322, s32[]{:T(128)} %get-tuple-element.321, f32[2,1024,2,256]{3,1,2,0:T(8,128)} %fusion.227, bf16[6144,2,256]{2,0,1:T(8,128)(2,1)} %get-tuple-element.342, f32[2,1024,2,6144]{3,1,2,0:T(8,128)} %get-tuple-element.306, ...), kind=kOutput, calls=%fused_computation.24.clone.1 | convolution fusion | flops 12986613760 | bytes 115366400 | tf_op jit(solution)/shard_map/while/body/eval_jaxpr/qkgt,tkd->qkgd/dot_general | solution.py:93
  1361.9 10.5 bitcast_reduce_fusion.5
  1373.0 38.0 %bitcast_reduce_fusion.6 = (f32[1024,2,2]{0,2,1:T(2,128)S(1)}, f32[2,1024,2,6144]{3,1,2,0:T(8,128)}) fusion(pred[6144]{0:T(1024)(128)(4,1)S(1)} %add_compare_fusion.2, bf16[6144,2,256]{2,0,1:T(8,128)(2,1)} %get-tuple-element.339, bf16[4,1024,2,2,256]{4,1,3,2,0:T(8,128)(2,1)} %get-tuple-element.338, s32[]{:T(128)} %get-tuple-element.321), kind=kOutput, calls=%fused_computation.3.clone.1 | convolution fusion | flops 12960395264 | bytes 109074944 | tf_op jit(solution)/shard_map/while/body/eval_jaxpr/qkgd,tkd->qkgt/dot_general | solution.py:84
  1411.0 31.3 %fusion.228 = f32[1024,2,2]{0,2,1:T(2,128)S(1)} fusion(f32[2,1024,2,6144]{3,1,2,0:T(8,128)} %get-tuple-element.306, f32[1024,2,2]{0,2,1:T(2,128)S(1)} %max.19, pred[6144]{0:T(1024)(128)(4,1)S(1)} %add_compare_fusion.2), kind=kLoop, calls=%fused_computation.6.clone.1 | loop fusion | flops 100659200 | bytes 100702208 | tf_op jit(solution)/shard_map/while/body/eval_jaxpr/reduce_sum | solution.py:92
  1450.2 13.2 fusion.227
  1463.4 38.8 %bitcast_dynamic-update-slice_fusion.2 = f32[4,1024,2,2,256]{4,1,3,2,0:T(8,128)} fusion(f32[4,1024,2,2,256]{4,1,3,2,0:T(8,128)} %get-tuple-element.322, s32[]{:T(128)} %get-tuple-element.321, f32[2,1024,2,256]{3,1,2,0:T(8,128)} %fusion.227, bf16[6144,2,256]{2,0,1:T(8,128)(2,1)} %get-tuple-element.342, f32[2,1024,2,6144]{3,1,2,0:T(8,128)} %get-tuple-element.306, ...), kind=kOutput, calls=%fused_computation.24.clone.1 | convolution fusion | flops 12986613760 | bytes 115366400 | tf_op jit(solution)/shard_map/while/body/eval_jaxpr/qkgt,tkd->qkgd/dot_general | solution.py:93
  1509.4 8.6 all-to-all-start
  1518.1 181.0 %all-to-all-done = f32[4,1024,2,2,256]{4,1,3,2,0:T(8,128)} async-done(((f32[4,1024,2,2,256]{4,1,3,2,0:T(8,128)}), f32[4,1024,2,2,256]{4,1,3,2,0:T(8,128)}, u32[]{:S(2)}, u32[]{:S(2)}) %all-to-all-start) | async-done | bytes 16777248 | tf_op jit(solution)/shard_map/all_to_all | solution.py:119
  1709.8 14.1 fusion.129
  1724.0 274.0 %all-reduce.9.cloned.1.call-done = bf16[1024,3840]{1,0:T(8,128)(2,1)} async-done(((bf16[1024,3840]{1,0:T(8,128)(2,1)}), bf16[1024,3840]{1,0:T(8,128)(2,1)}) %all-reduce.9.cloned.1.call-update) | async-done | bytes 7864336 | tf_op jit(solution)/shard_map/psum | solution.py:40
  2010.6 39.4 %fusion.46 = f32[1024,3840]{1,0:T(8,128)} fusion(bf16[2,3840,3840]{2,1,0:T(8,128)(2,1)} %param.27, bf16[1024,3840]{1,0:T(8,128)(2,1)S(1)} %get-tuple-element.179, f32[3840]{0:T(1024)S(1)} %copy-done.21, f32[1024]{0:T(1024)S(1)} %add_rsqrt_fusion.5), kind=kOutput, calls=%fused_computation.54 | convolution fusion | flops 30214717440 | bytes 53103616 | tf_op jit(solution)/shard_map/dot_general | solution.py:43
  2050.0 39.2 %fusion.105 = bf16[1024,3840]{1,0:T(8,128)(2,1)} fusion(f32[1024,3840]{1,0:T(8,128)} %fusion.46, bf16[2,3840,3840]{2,1,0:T(8,128)(2,1)} %param.28, bf16[1024,3840]{1,0:T(8,128)(2,1)S(1)} %get-tuple-element.179, f32[3840]{0:T(1024)S(1)} %copy-done.21, f32[1024]{0:T(1024)S(1)} %add_rsqrt_fusion.5), kind=kOutput, calls=%fused_computation.138 | convolution fusion | flops 30254039040 | bytes 60967936 | tf_op jit(solution)/shard_map/dot_general | solution.py:44
  2089.2 37.8 %fusion.135 = bf16[1024,3840]{1,0:T(8,128)(2,1)} fusion(bf16[1024,3840]{1,0:T(8,128)(2,1)} %fusion.105, bf16[2,3840,3840]{2,1,0:T(8,128)(2,1)} %param.29), kind=kOutput, calls=%fused_computation.160 | convolution fusion | flops 30202920960 | bytes 45219840 | tf_op jit(solution)/shard_map/dot_general | solution.py:46
  2137.0 261.9 %all-reduce.11.cloned.1.call-done = bf16[1024,3840]{1,0:T(8,128)(2,1)} async-done(((bf16[1024,3840]{1,0:T(8,128)(2,1)}), bf16[1024,3840]{1,0:T(8,128)(2,1)}) %all-reduce.11.cloned.1.call-update) | async-done | bytes 7864336 | tf_op jit(solution)/shard_map/psum | solution.py:46
  2404.4 8.7 fusion.96
  (201 shorter events, 197.4 us)
Async XLA Ops:
  7.2 439.5 %all-reduce.5.cloned.1.call-start = ((), (), s32[]{:S(2)}) async-start(), calls=%async_computation.2 | async-start | bytes 15728640 | tf_op jit(solution)/shard_map/psum | solution.py:40
  7.2 7.4 copy-start.11
  9.4 14.9 copy-start.24
  14.6 9.8 copy-start.29
  24.3 8.3 copy-start.28
  32.6 1.3 copy-start.10
  39.8 18.9 slice-start
  43.8 15.0 slice-start.1
  43.8 15.0 slice-start.2
  43.8 15.0 slice-start.3
  43.8 66.8 %collective-permute-start.1 = (bf16[1024,2,256]{0,2,1:T(8,128)(2,1)}, bf16[1024,2,256]{0,2,1:T(8,128)(2,1)}, u32[]{:S(2)}, u32[]{:S(2)}) collective-permute-start(bf16[1024,2,256]{0,2,1:T(8,128)(2,1)} %fusion.159), channel_id=1, source_target_pairs={{0,1},{1,2},{2,3},{4,5},{5,6},{6,7},{8,9},{9,10},{10,11},{12,13},{... | collective-permute-start | bytes 3145736 | tf_op jit(solution)/shard_map/ppermute | solution.py:61
  56.6 81.9 %collective-permute-start = (bf16[1024,2,256]{0,2,1:T(8,128)(2,1)}, bf16[1024,2,256]{0,2,1:T(8,128)(2,1)}, u32[]{:S(2)}, u32[]{:S(2)}) collective-permute-start(bf16[1024,2,256]{0,2,1:T(8,128)(2,1)} %bitcast.281), channel_id=1, source_target_pairs={{0,1},{1,2},{2,3},{4,5},{5,6},{6,7},{8,9},{9,10},{10,11},{12,13},{... | collective-permute-start | bytes 3145736 | tf_op jit(solution)/shard_map/ppermute | solution.py:61
  64.8 10.6 copy-start.25
  64.8 10.6 copy-start.30
  88.6 2.0 copy-start.7
  90.6 3.1 copy-start.14
  171.7 279.9 %copy-start.19 = (f32[3840]{0:T(1024)S(1)}, f32[3840]{0:T(1024)}, u32[]{:S(2)}) copy-start(f32[3840]{0:T(1024)} %get-tuple-element.151) | copy-start | bytes 46084
  171.7 675.5 %all-reduce.7.cloned.1.call-start = ((), (), s32[]{:S(2)}) async-start(), calls=%async_computation.3 | async-start | bytes 15728640 | tf_op jit(solution)/shard_map/psum | solution.py:46
  446.6 5.5 copy-start.4
  452.1 7.0 copy-start.23
  459.0 39.4 %copy-start.1 = (bf16[1024,3840]{1,0:T(8,128)(2,1)}, bf16[1024,3840]{1,0:T(8,128)(2,1)S(1)}, u32[]{:S(2)}) copy-start(bf16[1024,3840]{1,0:T(8,128)(2,1)S(1)} %get-tuple-element.183) | copy-start | bytes 23592964
  575.4 357.8 %all-gather.2.cloned.1.call-start = ((), (), s32[]{:S(2)}) async-start(), calls=%async_computation.4 | async-start | bytes 10485760 | tf_op jit(solution)/shard_map/all_gather | solution.py:109
  586.1 266.1 %copy-start.18 = (f32[3840]{0:T(1024)S(1)}, f32[3840]{0:T(1024)}, u32[]{:S(2)}) copy-start(f32[3840]{0:T(1024)} %get-tuple-element.149) | copy-start | bytes 46084
  847.3 5.5 copy-start.2
  847.3 13.0 slice-start.4
  852.7 7.6 slice-start.5
  852.7 7.6 copy-start.22
  860.3 8.6 copy-start
  860.3 8.5 copy-start.27
  904.5 9.6 copy-start.12
  905.9 8.3 copy-start.26
  915.4 17.8 copy-start.8
  1015.9 7.9 copy-start.16
  1158.0 7.9 copy-start.16
  1300.2 7.9 copy-start.16
  1442.3 7.9 copy-start.16
  1509.4 189.7 %all-to-all-start = ((f32[4,1024,2,2,256]{4,1,3,2,0:T(8,128)}), f32[4,1024,2,2,256]{4,1,3,2,0:T(8,128)}, u32[]{:S(2)}, u32[]{:S(2)}) async-start(f32[4,1024,2,2,256]{4,1,3,2,0:T(8,128)} %get-tuple-element.63), calls=%async_computation | async-start | bytes 33554432 | tf_op jit(solution)/shard_map/all_to_all | solution.py:119
  1518.0 480.0 %all-reduce.9.cloned.1.call-start = ((), (), s32[]{:S(2)}) async-start(), calls=%async_computation.5 | async-start | bytes 15728640 | tf_op jit(solution)/shard_map/psum | solution.py:40
  1723.9 279.0 %copy-start.17 = (f32[3840]{0:T(1024)S(1)}, f32[3840]{0:T(1024)}, u32[]{:S(2)}) copy-start(f32[3840]{0:T(1024)} %get-tuple-element.147) | copy-start | bytes 46084
  1724.0 675.0 %all-reduce.11.cloned.1.call-start = ((), (), s32[]{:S(2)}) async-start(), calls=%async_computation.6 | async-start | bytes 15728640 | tf_op jit(solution)/shard_map/psum | solution.py:46
  1998.0 5.5 copy-start.3
  2003.4 7.1 copy-start.21
  2010.6 39.4 %copy-start.5 = (bf16[1024,3840]{1,0:T(8,128)(2,1)}, bf16[1024,3840]{1,0:T(8,128)(2,1)S(1)}, u32[]{:S(2)}) copy-start(bf16[1024,3840]{1,0:T(8,128)(2,1)S(1)} %get-tuple-element.179) | copy-start | bytes 23592964
  2127.1 3.9 copy-start.15
  2127.1 5.9 copy-start.13
  2127.1 7.9 copy-start.9
  2127.1 276.8 %copy-start.20 = (f32[3840]{0:T(1024)S(1)}, f32[3840]{0:T(1024)}, u32[]{:S(2)}) copy-start(f32[3840]{0:T(1024)} %get-tuple-element.146) | copy-start | bytes 46084
  2398.9 5.5 copy-start.6
Sparse Core Ops, SparseCore 0:
  171.8 274.7 all-reduce.4
  575.6 271.6 all-reduce.6
  876.9 56.2 all-gather.1
  1724.1 273.8 all-reduce.8
  2127.2 271.6 all-reduce.10
where the time goes:
time: 2430 us; the launch traced here: 2420 us
  waiting for transfers between devices  1270 us (52%)
  matrix products  767 us (32%)
  other arithmetic  260 us (11%)
  local copies, waits for them, and re-layouts  88 us (4%)
    psum x2, waiting for transfers between devices, finish(): lax.psum(jnp.dot(attn_out.reshape(row_count, -1), w_out, preferred_elemen...  549 us
    psum x2, waiting for transfers between devices, finish(): lax.psum(jnp.dot(hidden_act, w_down, preferred_element_type=jnp.float32)....  519 us
    all_to_all x1, waiting for transfers between devices, spread_attention(): got_out = lax.all_to_all(part_out, 'cp', 0, 0, tiled=True)  181 us
    reduce_sum x8, other arithmetic, partial_block(): row_sum = cache_exp.sum(axis=-1) + own_exp.sum(axis=-1)  156 us
    dot_general x4, matrix products, partial_block(): jnp.einsum('qkgt,tkd->qkgd', cache_exp.astype(jnp.bfloat16), cache_v, pre...  155 us
    dot_general x4, matrix products, partial_block(): jnp.einsum('qkgd,tkd->qkgt', block_q, cache_k, preferred_element_type=jnp...  152 us
    dot_general x2, matrix products, finish(): gate_proj = jnp.dot(normed, w_gate, preferred_element_type=jnp.float32)  78.8 us
    dot_general x2, matrix products, finish(): up_proj = jnp.dot(normed, w_up, preferred_element_type=jnp.float32)  78.5 us
  transfers between devices with their start and end apart: 8, of which 6 were waited for; matrix products, arithmetic and copies ran while one was open for 6% of the time, Pallas kernels for 0%

commit v1 on v0

v1 whole, which is shorter than its diff:
```python
import functools

import jax
import jax.numpy as jnp
from jax import lax
from jax.experimental import pallas as pl
from jax.experimental.pallas import tpu as pltpu
from jax.sharding import PartitionSpec as P

NORM_EPS = 1e-6
LOCAL_BASE = 10000.0
GLOBAL_BASE = 1000000.0
GLOBAL_DIV = 8.0
NEG_BIG = -1e30
HEAD = 256
TILE = 256
VMEM_LIMIT = 67_000_000
MESH = pl.DeviceIdType.MESH
F32 = jnp.float32
BF16 = jnp.bfloat16


def dot(a, b):
    return jnp.dot(a, b, preferred_element_type=F32)


def dot_t(a, b):
    return lax.dot_general(a, b, (((1,), (1,)), ((), ())), preferred_element_type=F32)


def unit_rms(values):
    return values * lax.rsqrt(jnp.mean(values * values, axis=-1, keepdims=True) + NORM_EPS)


def rope_tables(positions, rope_base, divisor):
    half = HEAD // 2
    inv_freq = 1.0 / (rope_base ** (jnp.arange(0, 2 * half, 2, dtype=F32) / (2 * half)))
    angles = (positions.astype(F32) / divisor)[:, None] * inv_freq[None, :]
    return jnp.cos(angles), jnp.sin(angles)


def enter(peers):
    barrier = pltpu.get_barrier_semaphore()
    for peer in peers:
        pl.semaphore_signal(barrier, inc=1, device_id=peer, device_id_type=MESH)
    pl.semaphore_wait(barrier, len(peers))


def front_kernel(layer, window, g_row, x_hbm, g_ref, qk_ref, cos_ref, sin_ref, wq_hbm, wk_hbm, wv_hbm, kc_hbm, vc_hbm, o_hbm, k_hbm, v_hbm, xv, h, wt, q_v, kall, vall, o_v, x_sem, w_sem, kv_sem, c_sem, s_sem, r_sem, o_sem):
    rows, dim = x_hbm.shape
    kv_cols = k_hbm.shape[1]
    n_kv = kv_cols // HEAD
    n_q = q_v.shape[1] // HEAD
    base = rows if window else 0
    n_tile = 2 * n_kv + n_q
    chunk = rows // 4

    def w_copies(j):
        return (
            (j < n_kv, wv_hbm, j, n_kv),
            ((j >= n_kv) & (j < 2 * n_kv), wk_hbm, j - n_kv, n_kv),
            ((j >= 2 * n_kv) & (j < n_tile), wq_hbm, j - 2 * n_kv, n_q),
        )

    def w_copy(w_hbm, i, slot):
        return pltpu.make_async_copy(w_hbm.at[layer, :, pl.ds(pl.multiple_of(i * HEAD, HEAD), HEAD)], wt.at[slot], w_sem.at[slot])

    def start_w(j):
        for cond, w_hbm, i, count in w_copies(j):
            pl.when(cond)(lambda w_hbm=w_hbm, i=i, count=count: w_copy(w_hbm, jnp.clip(i, 0, count - 1), j % 2).start())

    def wait_w(j):
        w_copy(wv_hbm, 0, j % 2).wait()

    x_dst = xv if window else h
    x_copies = [pltpu.make_async_copy(x_hbm.at[pl.ds(i * chunk, chunk)], x_dst.at[pl.ds(i * chunk, chunk)], x_sem.at[i]) for i in range(4)]
    for copy in x_copies:
        copy.start()
    start_w(jnp.int32(0))
    start_w(jnp.int32(1))
    if window:
        me = lax.axis_index('cp')
        size = lax.axis_size('cp')
        right = lax.rem(me + 1, size)
        left = lax.rem(me + size - 1, size)
        enter(({'cp': left}, {'cp': right}))
        first = me == 0
        c_copies = [pltpu.make_async_copy(kc_hbm, kall.at[pl.ds(0, rows)], c_sem.at[0]), pltpu.make_async_copy(vc_hbm, vall.at[pl.ds(0, rows)], c_sem.at[1])]
        for copy in c_copies:
            pl.when(first)(copy.start)
    for copy in x_copies:
        copy.wait()
    if window:
        def norm_rows(i, carry):
            part = pl.ds(pl.multiple_of(i * 16, 16), 16)
            h[part, :] = (unit_rms(xv[part, :].astype(F32)) * (1.0 + g_ref[g_row:g_row + 1, :])).astype(BF16)
            return carry
        lax.fori_loop(0, rows // 16, norm_rows, 0)

    def rope(acc, part, gain):
        scaled = unit_rms(acc) * gain
        cos = cos_ref[part, :]
        sin = sin_ref[part, :]
        low = scaled[:, :HEAD // 2]
        high = scaled[:, HEAD // 2:]
        return jnp.concatenate([low * cos - high * sin, high * cos + low * sin], axis=-1)

    def head_tile(j, finish_tile):
        wait_w(j)
        slot = j % 2

        def rows_step(i, carry):
            part = pl.ds(pl.multiple_of(i * chunk, chunk), chunk)
            finish_tile(i, part, dot(h[part, :], wt[slot]))
            return carry
        lax.fori_loop(0, 4, rows_step, 0)
        start_w(j + 2)

    def v_step(j, carry):
        def put(i, part, acc):
            vall[pl.ds(pl.multiple_of(base + i * chunk, chunk), chunk), pl.ds(pl.multiple_of(j * HEAD, HEAD), HEAD)] = acc.astype(BF16)
        head_tile(j, put)
        return carry
    lax.fori_loop(0, n_kv, v_step, 0)

    def k_step(j, carry):
        def put(i, part, acc):
            kall[pl.ds(pl.multiple_of(base + i * chunk, chunk), chunk), pl.ds(pl.multiple_of(j * HEAD, HEAD), HEAD)] = rope(acc, part, 1.0 + qk_ref[2 * layer + 1:2 * layer + 2, :]).astype(BF16)
        head_tile(j + n_kv, put)
        return carry
    lax.fori_loop(0, n_kv, k_step, 0)

    kv_out = [pltpu.make_async_copy(kall.at[pl.ds(base, rows)], k_hbm, kv_sem.at[0]), pltpu.make_async_copy(vall.at[pl.ds(base, rows)], v_hbm, kv_sem.at[1])]
    for copy in kv_out:
        copy.start()
    if window:
        sends = [pltpu.make_async_remote_copy(src_ref=buf.at[pl.ds(base, rows)], dst_ref=buf.at[pl.ds(0, rows)], send_sem=s_sem.at[i], recv_sem=r_sem.at[i], device_id={'cp': right}, device_id_type=MESH) for i, buf in enumerate((kall, vall))]
        last = me == size - 1
        for copy in sends:
            pl.when(jnp.logical_not(last))(copy.start)

    def q_step(j, carry):
        def put(i, part, acc):
            q_v[part, pl.ds(pl.multiple_of(j * HEAD, HEAD), HEAD)] = (rope(acc, part, 1.0 + qk_ref[2 * layer:2 * layer + 1, :]).astype(BF16).astype(F32) * (HEAD ** -0.5)).astype(BF16)
        head_tile(j + 2 * n_kv, put)
        return carry
    lax.fori_loop(0, n_q, q_step, 0)

    if not window:
        out = pltpu.make_async_copy(q_v, o_hbm, o_sem.at[0])
        out.start()
        for copy in kv_out:
            copy.wait()
        out.wait()
        return

    @pl.when(first)
    def _():
        for copy in c_copies:
            copy.wait()

    @pl.when(jnp.logical_not(first))
    def _():
        for copy in sends:
            copy.wait_recv()

    groups = n_q // n_kv
    span = rows + chunk

    def attend(i, carry):
        part = pl.ds(pl.multiple_of(i * chunk, chunk), chunk)
        keys = pl.ds(pl.multiple_of(i * chunk, chunk), span)
        row_id = lax.broadcasted_iota(jnp.int32, (chunk, span), 0)
        col_id = lax.broadcasted_iota(jnp.int32, (chunk, span), 1)
        seen = (col_id > row_id) & (col_id <= row_id + rows)
        for head in range(n_kv):
            key = kall[keys, head * HEAD:(head + 1) * HEAD]
            value = vall[keys, head * HEAD:(head + 1) * HEAD]
            for g in range(groups):
                cols = slice((head * groups + g) * HEAD, (head * groups + g + 1) * HEAD)
                scores = jnp.where(seen, dot_t(q_v[part, cols], key), NEG_BIG)
                top = jnp.max(scores, axis=-1, keepdims=True)
                prob = jnp.exp(scores - top)
                total = jnp.sum(prob, axis=-1, keepdims=True)
                o_v[part, cols] = (dot(prob.astype(BF16), value) / total).astype(BF16)
        return carry
    lax.fori_loop(0, 4, attend, 0)
    out = pltpu.make_async_copy(o_v, o_hbm, o_sem.at[0])
    out.start()

    @pl.when(jnp.logical_not(last))
    def _():
        for copy in sends:
            copy.wait_send()
    for copy in kv_out:
        copy.wait()
    out.wait()


def front(layer, window, g_row, x, gains, qk_gains, cos, sin, w_query, w_key, w_value, k_cache, v_cache, collective_id):
    rows, dim = x.shape
    q_cols = w_query.shape[2]
    kv_cols = w_key.shape[2]
    key_rows = 2 * rows if window else rows
    any_spec = pl.BlockSpec(memory_space=pl.ANY)
    vmem_spec = pl.BlockSpec(memory_space=pltpu.VMEM)
    x_rows = rows if window else 16
    return pl.pallas_call(
        functools.partial(front_kernel, layer, window, g_row),
        out_shape=(jax.ShapeDtypeStruct((rows, q_cols), BF16), jax.ShapeDtypeStruct((rows, kv_cols), BF16), jax.ShapeDtypeStruct((rows, kv_cols), BF16)),
        in_specs=[any_spec, vmem_spec, vmem_spec, vmem_spec, vmem_spec, any_spec, any_spec, any_spec, any_spec, any_spec],
        out_specs=(any_spec, any_spec, any_spec),
        scratch_shapes=[
            pltpu.VMEM((x_rows, dim), BF16),
            pltpu.VMEM((rows, dim), BF16),
            pltpu.VMEM((2, dim, HEAD), BF16),
            pltpu.VMEM((rows, q_cols), BF16),
            pltpu.VMEM((key_rows, kv_cols), BF16),
            pltpu.VMEM((key_rows, kv_cols), BF16),
            pltpu.VMEM((rows, q_cols) if window else (16, q_cols), BF16),
            pltpu.SemaphoreType.DMA((4,)),
            pltpu.SemaphoreType.DMA((2,)),
            pltpu.SemaphoreType.DMA((2,)),
            pltpu.SemaphoreType.DMA((2,)),
            pltpu.SemaphoreType.DMA((2,)),
            pltpu.SemaphoreType.DMA((2,)),
            pltpu.SemaphoreType.DMA((1,)),
        ],
        compiler_params=pltpu.CompilerParams(collective_id=collective_id if window else None, has_side_effects=window, vmem_limit_bytes=VMEM_LIMIT),
        name='front_window' if window else 'front_global',
    )(x, gains, qk_gains, cos, sin, w_query, w_key, w_value, k_cache, v_cache)


def global_kernel(key_block, p0_ref, q_ref, kown, vown, kall, vall, kn_hbm, vn_hbm, o_ref, kb, vb, kn, vn, m_ref, l_ref, acc_ref, b_sem, s_sem, r_sem, n_sem):
    rows, q_cols = q_ref.shape
    size, shard, kv_cols = kall.shape
    n_kv = kv_cols // HEAD
    groups = q_cols // kv_cols
    me = lax.axis_index('cp')
    mate = me + 1 - 2 * lax.rem(me, 2)
    across = lax.rem(me + 2, size)
    chunk = rows // 2
    blocks = size * shard // key_block
    per_shard = shard // key_block
    masked_blocks = -(-(shard // 2) // key_block)
    first_pos = p0_ref[0]

    def fetch(idx, op):
        b = lax.rem(idx, blocks)
        slot = lax.rem(idx, 2)
        s = b // per_shard
        part = pl.ds(pl.multiple_of(lax.rem(b, per_shard) * key_block, key_block), key_block)

        @pl.when(s == me)
        def _():
            for i, (src, dst) in enumerate(((kown, kb), (vown, vb))):
                getattr(pltpu.make_async_copy(src.at[part], dst.at[slot], b_sem.at[slot, i]), op)()

        @pl.when(s != me)
        def _():
            for i, (src, dst) in enumerate(((kall, kb), (vall, vb))):
                getattr(pltpu.make_async_copy(src.at[s, part], dst.at[slot], b_sem.at[slot, i]), op)()

    fetch(jnp.int32(0), 'start')
    own = [pltpu.make_async_copy(kn_hbm, kn.at[me], n_sem.at[0]), pltpu.make_async_copy(vn_hbm, vn.at[me], n_sem.at[1])]
    for copy in own:
        copy.start()
    enter(({'cp': mate}, {'cp': across}))

    def remote(src, dst, i, peer):
        return pltpu.make_async_remote_copy(src_ref=src, dst_ref=dst, send_sem=s_sem.at[i], recv_sem=r_sem.at[i], device_id={'cp': peer}, device_id_type=MESH)
    to_across = [remote(kn_hbm, kn.at[me], 0, across), remote(vn_hbm, vn.at[me], 1, across)]
    to_mate = [remote(kn_hbm, kn.at[me], 2, mate), remote(vn_hbm, vn.at[me], 3, mate)]
    relay = [remote(kn.at[across], kn.at[across], 4, mate), remote(vn.at[across], vn.at[across], 5, mate)]
    for copy in to_across + to_mate:
        copy.start()
    for copy in own:
        copy.wait()

    def block_step(c, keys, values, seen_of):
        part = pl.ds(pl.multiple_of(c * chunk, chunk), chunk)
        for head in range(n_kv):
            query = jnp.concatenate([q_ref[part, (head * groups + g) * HEAD:(head * groups + g + 1) * HEAD] for g in range(groups)], axis=0)
            key = keys(head)
            scores = dot_t(query, key)
            if seen_of is not None:
                scores = jnp.where(seen_of(scores.shape), scores, NEG_BIG)
            old = m_ref[head]
            new = jnp.maximum(old, jnp.max(scores, axis=-1, keepdims=True))
            decay = jnp.exp(old - new)
            prob = jnp.exp(scores - jnp.concatenate([new] * (scores.shape[1] // 128), axis=1))
            lanes = prob[:, :128]
            for i in range(1, scores.shape[1] // 128):
                lanes = lanes + prob[:, i * 128:(i + 1) * 128]
            l_ref[head] = l_ref[head] * decay + lanes
            m_ref[head] = new
            acc_ref[head] = acc_ref[head] * jnp.concatenate([decay] * (HEAD // 128), axis=1) + dot(prob.astype(BF16), values(head))

    def chunk_step(c, carry):
        m_ref[...] = jnp.full(m_ref.shape, NEG_BIG, F32)
        l_ref[...] = jnp.zeros(l_ref.shape, F32)
        acc_ref[...] = jnp.zeros(acc_ref.shape, F32)

        def cache_step(masked, b, carry):
            idx = c * blocks + b
            fetch(idx, 'wait')

            @pl.when(idx + 1 < 2 * blocks)
            def _():
                fetch(idx + 1, 'start')
            slot = lax.rem(idx, 2)

            def seen_of(shape):
                return lax.broadcasted_iota(jnp.int32, shape, 1) < first_pos - b * key_block
            block_step(c, lambda head: kb[slot, :, head * HEAD:(head + 1) * HEAD], lambda head: vb[slot, :, head * HEAD:(head + 1) * HEAD], seen_of if masked else None)
            return carry
        lax.fori_loop(0, blocks - masked_blocks, functools.partial(cache_step, False), 0)

        @pl.when(c == 0)
        def _():
            for copy in to_across:
                copy.wait()
            for copy in relay:
                copy.start()
        lax.fori_loop(blocks - masked_blocks, blocks, functools.partial(cache_step, True), 0)

        @pl.when(c == 0)
        def _():
            for copy in to_mate + relay:
                copy.wait()
        per_new = rows // key_block

        def new_slices(i):
            s = i // per_new
            part = pl.ds(pl.multiple_of(lax.rem(i, per_new) * key_block, key_block), key_block)
            return (lambda head: kn[s, part, head * HEAD:(head + 1) * HEAD], lambda head: vn[s, part, head * HEAD:(head + 1) * HEAD])

        def past_step(i, carry):
            keys, values = new_slices(i)
            block_step(c, keys, values, None)
            return carry
        lax.fori_loop(0, me * per_new, past_step, 0)

        def own_step(i, carry):
            keys, values = new_slices(me * per_new + i)

            def seen_of(shape):
                row_id = lax.rem(lax.broadcasted_iota(jnp.int32, shape, 0), chunk)
                return lax.broadcasted_iota(jnp.int32, shape, 1) - row_id <= c * chunk - i * key_block
            block_step(c, keys, values, seen_of)
            return carry
        lax.fori_loop(0, ((c + 1) * chunk + key_block - 1) // key_block, own_step, 0)

        part = pl.ds(pl.multiple_of(c * chunk, chunk), chunk)
        for head in range(n_kv):
            total = jnp.sum(l_ref[head], axis=-1, keepdims=True)
            result = (acc_ref[head] / total).astype(BF16)
            for g in range(groups):
                o_ref[part, (head * groups + g) * HEAD:(head * groups + g + 1) * HEAD] = result[g * chunk:(g + 1) * chunk]
        return carry
    lax.fori_loop(0, 2, chunk_step, 0)


def global_attention(first_pos, queries, k_own, v_own, k_all, v_all, k_new, v_new, collective_id):
    rows, q_cols = queries.shape
    size, shard, kv_cols = k_all.shape
    n_kv = kv_cols // HEAD
    groups = q_cols // kv_cols
    key_block = min(512, shard // 2, rows // 2)
    stack = rows // 2 * groups
    any_spec = pl.BlockSpec(memory_space=pl.ANY)
    vmem_spec = pl.BlockSpec(memory_space=pltpu.VMEM)
    return pl.pallas_call(
        functools.partial(global_kernel, key_block),
        out_shape=jax.ShapeDtypeStruct((rows, q_cols), BF16),
        in_specs=[pl.BlockSpec(memory_space=pltpu.SMEM), vmem_spec] + [any_spec] * 6,
        out_specs=vmem_spec,
        scratch_shapes=[
            pltpu.VMEM((2, key_block, kv_cols), BF16),
            pltpu.VMEM((2, key_block, kv_cols), BF16),
            pltpu.VMEM((size, rows, kv_cols), BF16),
            pltpu.VMEM((size, rows, kv_cols), BF16),
            pltpu.VMEM((n_kv, stack, 128), F32),
            pltpu.VMEM((n_kv, stack, 128), F32),
            pltpu.VMEM((n_kv, stack, HEAD), F32),
            pltpu.SemaphoreType.DMA((2, 2)),
            pltpu.SemaphoreType.DMA((6,)),
            pltpu.SemaphoreType.DMA((6,)),
            pltpu.SemaphoreType.DMA((2,)),
        ],
        compiler_params=pltpu.CompilerParams(collective_id=collective_id, has_side_effects=True, vmem_limit_bytes=VMEM_LIMIT),
        name='global_attention',
    )(first_pos, queries, k_own, v_own, k_all, v_all, k_new, v_new)


N_CHUNK = 4
N_SUB = 4
RECV_SLOTS = 4


def back_kernel(layer, gather, *refs):
    if gather:
        (o_hbm, x_hbm, g_ref, wo_hbm, wg_hbm, wu_hbm, wd_hbm, kown, vown, xo_hbm, ho_hbm, kall, vall) = refs[:13]
        refs = refs[13:]
    else:
        (o_hbm, x_hbm, g_ref, wo_hbm, wg_hbm, wu_hbm, wd_hbm, xo_hbm) = refs[:8]
        refs = refs[8:]
    (part, tot, xv, u, wo_v, o_v, hact, gu, dn, recv2, wo_sem, ld_sem, gu_sem, dn_sem, s1, s2s, s2r, s3, credit, out_sem) = refs[:20]
    rows, dim = x_hbm.shape
    ff = wg_hbm.shape[2]
    chunk = rows // N_CHUNK
    sub = chunk // N_SUB
    per = N_CHUNK * N_SUB
    n_ev = 2 * per
    n_dim = dim // TILE
    n_ff = ff // TILE
    tp = lax.axis_index('tp')
    outer = (tp == 0) | (tp == 3)
    inner = jnp.logical_not(outer)
    mate = tp + 1 - 2 * lax.rem(tp, 2)
    middle = 3 - tp

    def cols(t):
        return pl.ds(pl.multiple_of(t * TILE, TILE), TILE)

    def rows_of(n):
        return pl.ds(pl.multiple_of(lax.rem(n, per) * sub, sub), sub)

    def wo_copy(t):
        return pltpu.make_async_copy(wo_hbm.at[layer, :, cols(t)], wo_v.at[:, cols(t)], wo_sem.at[t])

    def gu_copies(i):
        slot = lax.rem(i, 2)
        t = lax.rem(i, n_ff)
        return [pltpu.make_async_copy(w.at[layer, :, cols(t)], gu.at[slot, k], gu_sem.at[slot, k]) for k, w in enumerate((wg_hbm, wu_hbm))]

    def dn_copy(i):
        slot = lax.rem(i, 2)
        return pltpu.make_async_copy(wd_hbm.at[layer, :, cols(lax.rem(i, n_dim))], dn.at[slot], dn_sem.at[slot])

    o_copy = pltpu.make_async_copy(o_hbm, o_v, ld_sem.at[0])
    x_copy = pltpu.make_async_copy(x_hbm, xv, ld_sem.at[1])
    o_copy.start()
    for t in range(n_dim):
        wo_copy(t).start()
    x_copy.start()
    for i in range(2):
        for copy in gu_copies(jnp.int32(i)):
            copy.start()
        dn_copy(jnp.int32(i)).start()

    peers = [{'tp': mate}, {'tp': middle}]
    if gather:
        g_s, g_r = refs[20:22]
        size = lax.axis_size('cp')
        cp = lax.axis_index('cp')
        near = cp + 1 - 2 * lax.rem(cp, 2)
        across = lax.rem(cp + 2, size)
        peers += [{'cp': near}, {'cp': across}]
    enter(peers)
    if gather:
        def remote(src, dst, i, peer):
            return pltpu.make_async_remote_copy(src_ref=src, dst_ref=dst, send_sem=g_s.at[i], recv_sem=g_r.at[i], device_id={'cp': peer}, device_id_type=MESH)
        to_across = [remote(kown, kall.at[cp], 0, across), remote(vown, vall.at[cp], 1, across)]
        to_near = [remote(kown, kall.at[cp], 2, near), remote(vown, vall.at[cp], 3, near)]
        relay = [remote(kall.at[across], kall.at[across], 4, near), remote(vall.at[across], vall.at[across], 5, near)]
        for copy in to_across + to_near:
            copy.start()

    def hop1(n):
        return pltpu.make_async_remote_copy(src_ref=part.at[rows_of(n)], dst_ref=tot.at[rows_of(n)], send_sem=s1.at[n], recv_sem=s1.at[n], device_id={'tp': mate}, device_id_type=MESH)

    def hop2(n):
        return pltpu.make_async_remote_copy(src_ref=part.at[rows_of(n)], dst_ref=recv2.at[lax.rem(n, RECV_SLOTS)], send_sem=s2s.at[n], recv_sem=s2r.at[n], device_id={'tp': middle}, device_id_type=MESH)

    def hop3(n):
        return pltpu.make_async_remote_copy(src_ref=tot.at[rows_of(n)], dst_ref=tot.at[rows_of(n)], send_sem=s3.at[n], recv_sem=s3.at[n], device_id={'tp': mate}, device_id_type=MESH)

    def out_copies(n):
        m = lax.rem(n, per)
        made = [pltpu.make_async_copy(xv.at[rows_of(n)], xo_hbm.at[rows_of(n)], out_sem.at[0, m])]
        if gather:
            made.append(pltpu.make_async_copy(u.at[rows_of(n)], ho_hbm.at[rows_of(n)], out_sem.at[1, m]))
        return made

    def send_chunk(first):
        @pl.when(outer)
        def _():
            for i in range(N_SUB):
                hop1(first + i).start()

    def normalize(n):
        start = lax.rem(n, per) * sub
        step = min(16, sub)

        @pl.when(n < per)
        def _():
            def body(i, carry):
                r = pl.ds(pl.multiple_of(start + i * step, step), step)
                x1 = (xv[r, :].astype(F32) + unit_rms(tot[r, :].astype(F32)) * (1.0 + g_ref[4 * layer + 1:4 * layer + 2, :])).astype(BF16)
                xv[r, :] = x1
                u[r, :] = (unit_rms(x1.astype(F32)) * (1.0 + g_ref[4 * layer + 2:4 * layer + 3, :])).astype(BF16)
                return carry
            lax.fori_loop(0, sub // step, body, 0)

        @pl.when(n >= per)
        def _():
            def body(i, carry):
                r = pl.ds(pl.multiple_of(start + i * step, step), step)
                x2 = (xv[r, :].astype(F32) + unit_rms(tot[r, :].astype(F32)) * (1.0 + g_ref[4 * layer + 3:4 * layer + 4, :])).astype(BF16)
                xv[r, :] = x2
                if gather:
                    u[r, :] = (unit_rms(x2.astype(F32)) * (1.0 + g_ref[4 * layer + 4:4 * layer + 5, :])).astype(BF16)
                return carry
            lax.fori_loop(0, sub // step, body, 0)
            for copy in out_copies(n):
                copy.start()

    def event(tick):
        @pl.when(inner)
        def _():
            n = tick

            @pl.when((n >= 0) & (n < n_ev))
            def _():
                hop1(n).wait_recv()
                r = rows_of(n)
                part[r, :] = (part[r, :].astype(F32) + tot[r, :].astype(F32)).astype(BF16)

                @pl.when(n >= RECV_SLOTS)
                def _():
                    pl.semaphore_wait(credit, 1)
            k = tick - 1

            @pl.when((k >= 0) & (k < n_ev))
            def _():
                hop2(k).wait_recv()
                hop2(k).wait_send()
                r = rows_of(k)
                tot[r, :] = (part[r, :].astype(F32) + recv2[lax.rem(k, RECV_SLOTS)].astype(F32)).astype(BF16)

                @pl.when(k < n_ev - RECV_SLOTS)
                def _():
                    pl.semaphore_signal(credit, inc=1, device_id={'tp': middle}, device_id_type=MESH)

            @pl.when((n >= 0) & (n < n_ev))
            def _():
                hop2(n).start()

            @pl.when((k >= 0) & (k < n_ev))
            def _():
                @pl.when(k >= 1)
                def _():
                    hop3(k - 1).wait_send()
                normalize(k)
                hop3(k).start()

        @pl.when(outer)
        def _():
            n = tick - 2

            @pl.when((n >= 0) & (n < n_ev))
            def _():
                hop1(n).wait_send()
                hop3(n).wait_recv()
                normalize(n)

    o_copy.wait()

    def wo_chunk(c, carry):
        r = pl.ds(pl.multiple_of(c * chunk, chunk), chunk)

        def tile(t, carry):
            @pl.when(c == 0)
            def _():
                wo_copy(t).wait()
            part[r, cols(t)] = dot(o_v[r, :], wo_v[:, cols(t)]).astype(BF16)
            return carry
        lax.fori_loop(0, n_dim, tile, 0)
        send_chunk(c * N_SUB)
        return carry
    lax.fori_loop(0, N_CHUNK, wo_chunk, 0)
    x_copy.wait()

    lead = N_SUB + 2

    def tick_only(tick, carry):
        event(tick)
        return carry
    lax.fori_loop(0, lead, tick_only, 0)
    ticks_per = N_SUB + 1
    tasks = n_ff + n_dim
    stride = -(-tasks // ticks_per)

    def ffn_chunk(c, carry):
        r = pl.ds(pl.multiple_of(c * chunk, chunk), chunk)

        def task(t, carry):
            @pl.when(t < n_ff)
            def _():
                i = c * n_ff + t
                for copy in gu_copies(i):
                    copy.wait()
                slot = lax.rem(i, 2)
                lhs = u[r, :]
                gate = dot(lhs, gu[slot, 0])
                up = dot(lhs, gu[slot, 1])
                hact[:, cols(t)] = (jax.nn.gelu(gate, approximate=True) * up).astype(BF16)

                @pl.when(i + 2 < N_CHUNK * n_ff)
                def _():
                    for copy in gu_copies(i + 2):
                        copy.start()

            @pl.when(t >= n_ff)
            def _():
                i = c * n_dim + t - n_ff
                dn_copy(i).wait()
                part[r, cols(t - n_ff)] = dot(hact[...], dn[lax.rem(i, 2)]).astype(BF16)

                @pl.when(i + 2 < N_CHUNK * n_dim)
                def _():
                    dn_copy(i + 2).start()

            @pl.when(lax.rem(t, stride) == stride - 1)
            def _():
                event(lead + c * ticks_per + t // stride)
            return carry
        lax.fori_loop(0, tasks, task, 0)
        send_chunk(per + c * N_SUB)
        return carry
    lax.fori_loop(0, N_CHUNK, ffn_chunk, 0)
    done = lead + N_CHUNK * (tasks // stride)
    if gather:
        for copy in to_across:
            copy.wait()
        for copy in relay:
            copy.start()
    lax.fori_loop(done, n_ev + 2, tick_only, 0)

    @pl.when(inner)
    def _():
        hop3(n_ev - 1).wait_send()

    def finish(m, carry):
        for copy in out_copies(m):
            copy.wait()
        return carry
    lax.fori_loop(0, per, finish, 0)
    if gather:
        for copy in to_near + relay:
            copy.wait()


def back(layer, attn_out, hidden, gains, w_out, w_gate, w_up, w_down, cache, collective_id):
    rows, dim = hidden.shape
    q_cols = attn_out.shape[1]
    ff = w_gate.shape[2]
    chunk = rows // N_CHUNK
    sub = chunk // N_SUB
    gather = cache is not None
    any_spec = pl.BlockSpec(memory_space=pl.ANY)
    vmem_spec = pl.BlockSpec(memory_space=pltpu.VMEM)
    n_ev = 2 * N_CHUNK * N_SUB
    args = [attn_out, hidden, gains, w_out, w_gate, w_up, w_down]
    outs = [jax.ShapeDtypeStruct((rows, dim), BF16)]
    scratch = [
        pltpu.VMEM((rows, dim), BF16),
        pltpu.VMEM((rows, dim), BF16),
        pltpu.VMEM((rows, dim), BF16),
        pltpu.VMEM((rows, dim), BF16),
        pltpu.VMEM((q_cols, dim), BF16),
        pltpu.VMEM((rows, q_cols), BF16),
        pltpu.VMEM((chunk, ff), BF16),
        pltpu.VMEM((2, 2, dim, TILE), BF16),
        pltpu.VMEM((2, ff, TILE), BF16),
        pltpu.VMEM((RECV_SLOTS, sub, dim), BF16),
        pltpu.SemaphoreType.DMA((dim // TILE,)),
        pltpu.SemaphoreType.DMA((2,)),
        pltpu.SemaphoreType.DMA((2, 2)),
        pltpu.SemaphoreType.DMA((2,)),
        pltpu.SemaphoreType.DMA((n_ev,)),
        pltpu.SemaphoreType.DMA((n_ev,)),
        pltpu.SemaphoreType.DMA((n_ev,)),
        pltpu.SemaphoreType.DMA((n_ev,)),
        pltpu.SemaphoreType.REGULAR,
        pltpu.SemaphoreType.DMA((2, N_CHUNK * N_SUB)),
    ]
    if gather:
        shard, kv_cols = cache[0].shape
        args += list(cache)
        outs += [jax.ShapeDtypeStruct((rows, dim), BF16)] + [jax.ShapeDtypeStruct((4, shard, kv_cols), BF16)] * 2
        scratch += [pltpu.SemaphoreType.DMA((6,)), pltpu.SemaphoreType.DMA((6,))]
    return pl.pallas_call(
        functools.partial(back_kernel, layer, gather),
        out_shape=tuple(outs),
        in_specs=[any_spec, any_spec, vmem_spec] + [any_spec] * (len(args) - 3),
        out_specs=tuple([any_spec] * len(outs)),
        scratch_shapes=scratch,
        compiler_params=pltpu.CompilerParams(collective_id=collective_id, has_side_effects=True, vmem_limit_bytes=VMEM_LIMIT),
        name='back_%d' % layer,
    )(*args)


def solution(mesh):
    row_spec = P(('dp', 'cp'), None)
    cache_spec = P(('dp', 'cp'), 'tp', None)
    window_spec = P('dp', 'tp', None)
    col_spec = P(None, None, 'tp')
    row_split = P(None, 'tp', None)
    replicated = P()

    def device_step(hidden, start_pos, k_local, v_local, k_global, v_global, w_query, w_key, w_value, w_out, w_gate, w_up, w_down, norm_gain, qk_gain):
        first_pos = start_pos[0]
        cp_index = lax.axis_index('cp')
        rows, dim = hidden.shape
        window = k_local.shape[0]
        flat = lambda a: a.reshape(a.shape[0], -1)
        positions = first_pos + cp_index * rows + jnp.arange(rows)
        gains = jnp.concatenate([norm_gain.reshape(8, dim), jnp.zeros((8, dim), F32)], axis=0)
        qk_gains = jnp.concatenate([qk_gain.reshape(4, HEAD), jnp.zeros((4, HEAD), F32)], axis=0)
        turn = jnp.remainder(first_pos, window)
        rolled = [lax.dynamic_slice_in_dim(jnp.concatenate([flat(a), flat(a)], axis=0), turn, window, axis=0) for a in (k_local, v_local)]
        cos, sin = rope_tables(positions, LOCAL_BASE, 1.0)
        attn, key_loc, value_loc = front(0, True, 0, hidden, gains, qk_gains, cos, sin, w_query, w_key, w_value, rolled[0], rolled[1], 0)
        cache = (flat(k_global), flat(v_global))
        middle, normed, k_all, v_all = back(0, attn, hidden, gains, w_out, w_gate, w_up, w_down, cache, 1)
        cos, sin = rope_tables(positions, GLOBAL_BASE, GLOBAL_DIV)
        queries, key_glob, value_glob = front(1, False, 4, normed, gains, qk_gains, cos, sin, w_query, w_key, w_value, rolled[0], rolled[1], None)
        attn = global_attention(start_pos, queries, cache[0], cache[1], k_all, v_all, key_glob, value_glob, 2)
        final, = back(1, attn, middle, gains, w_out, w_gate, w_up, w_down, None, 3)
        shaped = lambda a: a.reshape(rows, -1, HEAD)
        return final, shaped(key_loc), shaped(value_loc), shaped(key_glob), shaped(value_glob)

    return jax.shard_map(device_step, mesh=mesh, in_specs=(row_spec, P('dp'), window_spec, window_spec, cache_spec, cache_spec, col_spec, col_spec, col_spec, row_split, col_spec, col_spec, row_split, replicated, replicated), out_specs=(row_spec, cache_spec, cache_spec, cache_spec, cache_spec), check_vma=False)
```

time: 2430 us -> 1160 us (0.48)
  waiting for transfers between devices: 1270 us -> 0 us
  Pallas kernels: 0 us -> 1110 us
  matrix products: 767 us -> 0 us
  other arithmetic: 260 us -> 10.1 us
  local copies, waits for them, and re-layouts: 88 us -> 32 us
    pallas_call x0 -> x5, Pallas kernels: none -> 1110 us  [the longest x2 805 us: back(): pl.pallas_call(functools.partial(back_kernel, layer, gather), out_shape=t...]
    psum x4 -> x0, waiting for transfers between devices: 1070 us -> none  [the longest x2 549 us: finish(): lax.psum(jnp.dot(attn_out.reshape(row_count, -1), w_out, preferred_elemen...]
    dot_general x31 -> x0, matrix products: 740 us -> none  [the longest x4 155 us: partial_block(): jnp.einsum('qkgt,tkd->qkgd', cache_exp.astype(jnp.bfloat16), cache_v, pre...]
    reduce_sum x18 -> x0, other arithmetic: 210 us -> none  [the longest x8 156 us: partial_block(): row_sum = cache_exp.sum(axis=-1) + own_exp.sum(axis=-1)]
    all_to_all x1 -> x0, waiting for transfers between devices: 181 us -> none  [spread_attention(): got_out = lax.all_to_all(part_out, 'cp', 0, 0, tiled=True)]
    dot_general x6 -> x0, local copies, waits for them, and re-layouts: 43.5 us -> none  [the longest x3 27.2 us: project(): jnp.dot(normed, w_query, preferred_element_type=jnp.float32)]
    sub x1 -> x0, matrix products: 27.8 us -> none  [window_attention(): attn_prob = jax.nn.softmax(scores, axis=-1).astype(jnp.bfloat16)]
  transfers between devices with their start and end apart: 8 -> 0, of which waited for: 6 -> 0; matrix products, arithmetic and copies ran while one was open for 6% -> 0% of each run, Pallas kernels for 0% -> 0%
where the time goes in v1:
time: 1160 us; the launch traced here: 1150 us
  Pallas kernels  1110 us (96%)
  local copies, waits for them, and re-layouts  32 us (3%)
    pallas_call x2, Pallas kernels, back(): pl.pallas_call(functools.partial(back_kernel, layer, gather), out_shape=t...  805 us
    pallas_call x1, Pallas kernels, global_attention(): pl.pallas_call(functools.partial(global_kernel, key_block), out_shape=jax...  215 us
    pallas_call x2, Pallas kernels, front(): pl.pallas_call(functools.partial(front_kernel, layer, window, g_row), out...  91 us

profile of v1, /device:TPU:4, one launch (start us, length us, event | category | flops | bytes accessed | tf_op | source)
XLA Modules:
  0.0 1154.5 jit_solution(16308637763405602975)
XLA Ops:
  1.3 0.7 reshape.60
  2.0 0.6 concatenate.13.qk_ref
  2.7 0.9 reshape.59
  3.6 0.7 concatenate.12.g_ref.refs_2_
  4.3 3.0 multiply_sine_fusion.1
  7.4 3.0 multiply_sine_fusion
  10.4 1.4 copy.20
  11.8 1.4 copy.21
  13.3 4.0 fusion
  17.3 59.9 %front_window.1 = (bf16[1024,1024]{1,0:T(8,128)(2,1)}, bf16[1024,512]{1,0:T(8,128)(2,1)}, bf16[1024,512]{1,0:T(8,128)(2,1)}) custom-call(bf16[1024,3840]{1,0:T(8,128)(2,1)} %refs_1_.1, f32[16,3840]{1,0:T(8,128)} %concatenate.12.g_ref.refs_2_, f32[8,256]{1,0:T(8,128)} %concatenate.13.qk_ref, f32[1024,128]{1,0:T(8,128)} %get-tuple-element.28.cos_ref, ...), custom_call_target="tpu_custom_call" | custom-call | tf_op jit(solution)/shard_map/front_window/pallas_call | solution.py:208
  77.1 2.1 reshape.65
  79.3 0.0 slice-start
  79.3 2.3 reshape.66
  81.6 0.0 slice-start.1
  81.6 6.7 copy.22
  88.3 0.0 slice-done
  88.3 0.0 slice-done.1
  88.3 3.7 copy.23
  92.0 404.9 %back_0.1 = (bf16[1024,3840]{1,0:T(8,128)(2,1)}, bf16[1024,3840]{1,0:T(8,128)(2,1)}, bf16[4,6144,512]{2,1,0:T(8,128)(2,1)}, bf16[4,6144,512]{2,1,0:T(8,128)(2,1)}) custom-call(bf16[1024,1024]{1,0:T(8,128)(2,1)} %get-tuple-element.15.refs_0_, bf16[1024,3840]{1,0:T(8,128)(2,1)} %refs_1_.1, f32[16,3840]{1,0:T(8,128)} %concatenate.12.g_ref.refs_2_, ...), custom_call_target="tpu_custom_call" | custom-call | tf_op jit(solution)/shard_map/back_0/pallas_call | solution.py:694
  496.9 31.1 %front_global.1 = (bf16[1024,1024]{1,0:T(8,128)(2,1)}, bf16[1024,512]{1,0:T(8,128)(2,1)}, bf16[1024,512]{1,0:T(8,128)(2,1)}) custom-call(bf16[1024,3840]{1,0:T(8,128)(2,1)} %get-tuple-element.16.x_hbm, f32[16,3840]{1,0:T(8,128)} %concatenate.12.g_ref.refs_2_, f32[8,256]{1,0:T(8,128)} %concatenate.13.qk_ref, f32[1024,128]{1,0:T(8,128)} %get-tuple-element.26.cos_ref, ...), custom_call_target="tpu_custom_call" | custom-call | tf_op jit(solution)/shard_map/front_global/pallas_call | solution.py:208
  528.0 215.3 %global_attention.1.refs_0_ = bf16[1024,1024]{1,0:T(8,128)(2,1)} custom-call(s32[1]{0:T(128)} %copy.25.p0_ref, bf16[1024,1024]{1,0:T(8,128)(2,1)} %get-tuple-element.17.q_ref, bf16[6144,512]{1,0:T(8,128)(2,1)} %bitcast.14, bf16[6144,512]{1,0:T(8,128)(2,1)} %bitcast.16, bf16[4,6144,512]{2,1,0:T(8,128)(2,1)} %get-tuple-element.18.kall, ...), custom_call_target="tpu_custom_call" | custom-call | tf_op jit(solution)/shard_map/global_attention/pallas_call | solution.py:373
  743.3 400.0 %back_1.1 = bf16[1024,3840]{1,0:T(8,128)(2,1)} custom-call(bf16[1024,1024]{1,0:T(8,128)(2,1)} %global_attention.1.refs_0_, bf16[1024,3840]{1,0:T(8,128)(2,1)} %get-tuple-element.22.refs_1_, f32[16,3840]{1,0:T(8,128)} %concatenate.12.g_ref.refs_2_, bf16[2,1024,3840]{2,1,0:T(8,128)(2,1)} %refs_3_.3, bf16[2,3840,3840]{2,1,0:T(8,128)(2,1)} %refs_4_.3, ...), custom_call_target="tpu_custom_call" | custom-call | tf_op jit(solution)/shard_map/back_1/pallas_call | solution.py:694
  1143.3 2.1 reshape.68
  1145.4 2.1 reshape.67
  1147.6 7.0 copy.26
  (5 shorter events, 0.0 us)
Async XLA Ops:
  79.3 9.0 slice-start
  81.6 6.7 slice-start.1

commit v2 on v0

v2 whole, which is shorter than its diff:
```python
import functools

import jax
import jax.numpy as jnp
from jax import lax
from jax.experimental import pallas as pl
from jax.experimental.pallas import tpu as pltpu
from jax.sharding import PartitionSpec as P

NORM_EPS = 1e-6
LOCAL_BASE = 10000.0
GLOBAL_BASE = 1000000.0
GLOBAL_DIV = 8.0
NEG_BIG = -1e30
HEAD = 256
TILE = 256
VMEM_LIMIT = 67_000_000
MESH = pl.DeviceIdType.MESH
F32 = jnp.float32
BF16 = jnp.bfloat16


def dot(a, b):
    return jnp.dot(a, b, preferred_element_type=F32)


def dot_t(a, b):
    return lax.dot_general(a, b, (((1,), (1,)), ((), ())), preferred_element_type=F32)


def unit_rms(values):
    return values * lax.rsqrt(jnp.mean(values * values, axis=-1, keepdims=True) + NORM_EPS)


def rope_tables(positions, rope_base, divisor):
    half = HEAD // 2
    inv_freq = 1.0 / (rope_base ** (jnp.arange(0, 2 * half, 2, dtype=F32) / (2 * half)))
    angles = (positions.astype(F32) / divisor)[:, None] * inv_freq[None, :]
    return jnp.cos(angles), jnp.sin(angles)


def enter(peers):
    barrier = pltpu.get_barrier_semaphore()
    for peer in peers:
        pl.semaphore_signal(barrier, inc=1, device_id=peer, device_id_type=MESH)
    pl.semaphore_wait(barrier, len(peers))


N_CHUNK = 4
N_SUB = 4
RECV_SLOTS = 4


def spread(count, weights):
    total, seen, marks = sum(weights), 0, []
    for i, weight in enumerate(weights):
        seen += weight
        if seen * count >= total * (len(marks) + 1):
            marks.append(i)
    return marks


def layer_kernel(layer, names, *refs):
    r = dict(zip(names, refs))
    first_layer = layer == 0
    x_hbm, g_ref, qk_ref = (r[n] for n in ('x', 'gains', 'qk_gains'))
    cos_ref, sin_ref = (r['cos'], r['sin']) if first_layer else (r['top'], r['sums'])
    part, tot, xv, wt, dn, wo_v, qo, hact, recv2 = (r[n] for n in ('part', 'tot', 'xv', 'wt', 'dn', 'wo_v', 'qo', 'hact', 'recv2'))
    rows, dim = x_hbm.shape
    ff = r['w_gate'].shape[2]
    kv_cols = r['w_key'].shape[2]
    q_cols = r['w_query'].shape[2]
    n_kv, n_q = kv_cols // HEAD, q_cols // HEAD
    groups = n_q // n_kv
    chunk = rows // N_CHUNK
    sub = chunk // N_SUB
    per = N_CHUNK * N_SUB
    n_ev = 2 * per
    n_dim, n_ff = dim // TILE, ff // TILE
    tp, cp, size = lax.axis_index('tp'), lax.axis_index('cp'), lax.axis_size('cp')
    outer = (tp == 0) | (tp == 3)
    inner = jnp.logical_not(outer)
    mate = tp + 1 - 2 * lax.rem(tp, 2)
    middle = 3 - tp
    near = cp + 1 - 2 * lax.rem(cp, 2)
    across = lax.rem(cp + 2, size)
    right, left = lax.rem(cp + 1, size), lax.rem(cp + size - 1, size)

    def aligned(start, length):
        return pl.ds(pl.multiple_of(start, length), length)

    def cols(t):
        return aligned(t * TILE, TILE)

    def chunk_rows(c):
        return aligned(c * chunk, chunk)

    def rows_of(n):
        return aligned(lax.rem(n, per) * sub, sub)

    n_tile = 2 * n_kv + n_q

    def start_w(j):
        for low, high, w_hbm in ((0, n_kv, r['w_value']), (n_kv, 2 * n_kv, r['w_key']), (2 * n_kv, n_tile, r['w_query'])):
            @pl.when((j >= low) & (j < high))
            def _():
                slot = lax.rem(j, 4)
                pltpu.make_async_copy(w_hbm.at[layer, :, cols(jnp.clip(j - low, 0, high - low - 1))], wt.at[slot], r['w_sem'].at[slot]).start()

    def wait_w(j):
        slot = lax.rem(j, 4)
        pltpu.make_async_copy(r['w_value'].at[layer, :, cols(0)], wt.at[slot], r['w_sem'].at[slot]).wait()

    def wo_copy(t):
        return pltpu.make_async_copy(r['w_out'].at[layer, :, cols(t)], wo_v.at[:, cols(t)], r['wo_sem'].at[t])

    def gu_copies(i):
        slot, t = lax.rem(i, 2) * 2, lax.rem(i, n_ff)
        return [pltpu.make_async_copy(r[w].at[layer, :, cols(t)], wt.at[slot + k], r['w_sem'].at[slot + k]) for k, w in enumerate(('w_gate', 'w_up'))]

    def dn_copy(i):
        slot = lax.rem(i, 2)
        return pltpu.make_async_copy(r['w_down'].at[layer, :, cols(lax.rem(i, n_dim))], dn.at[slot], r['dn_sem'].at[slot])

    h_src = x_hbm if first_layer else r['h']
    h_dst = xv if first_layer else part
    h_copies = [pltpu.make_async_copy(h_src.at[pl.ds(i * chunk, chunk)], h_dst.at[pl.ds(i * chunk, chunk)], r['h_sem'].at[i]) for i in range(N_CHUNK)]
    h_copies[0].start()
    start_w(jnp.int32(0))
    for copy in h_copies[1:]:
        copy.start()
    for j in range(1, 4):
        start_w(jnp.int32(j))
    if not first_layer:
        t_copies = [pltpu.make_async_copy(r[src], dst, r['own_sem'].at[i]) for i, (src, dst) in enumerate((('cos', cos_ref), ('sin', sin_ref)))]
        for copy in t_copies:
            copy.start()

    peers = [{'tp': mate}, {'tp': middle}, {'cp': near}, {'cp': across}]
    if first_layer:
        peers += [{'cp': left}, {'cp': right}]
    enter(peers)

    def to_cp(src, dst, kind, i, peer):
        return pltpu.make_async_remote_copy(src_ref=src, dst_ref=dst, send_sem=r[kind + '_s'].at[i], recv_sem=r[kind + '_r'].at[i], device_id={'cp': peer}, device_id_type=MESH)

    if first_layer:
        is_first, is_last = cp == 0, cp == size - 1
        old_copies = [pltpu.make_async_copy(r[old], r[buf].at[pl.ds(0, rows)], r['old_sem'].at[i]) for i, (old, buf) in enumerate((('k_old', 'keys'), ('v_old', 'values')))]

        @pl.when(is_first)
        def _():
            for copy in old_copies:
                copy.start()
        for i, copy in enumerate(h_copies):
            copy.wait()

            def norm_rows(k, carry):
                these = aligned(i * chunk + k * 16, 16)
                part[these, :] = (unit_rms(xv[these, :].astype(F32)) * (1.0 + g_ref[0:1, :])).astype(BF16)
                return carry
            lax.fori_loop(0, chunk // 16, norm_rows, 0)
        base = rows
    else:
        for copy in h_copies + t_copies:
            copy.wait()
        base = 0

    def rope(acc, these, gain):
        scaled = unit_rms(acc) * gain
        cos, sin = cos_ref[these, :], sin_ref[these, :]
        low, high = scaled[:, :HEAD // 2], scaled[:, HEAD // 2:]
        return jnp.concatenate([low * cos - high * sin, high * cos + low * sin], axis=-1)

    def head_tile(j, put):
        wait_w(j)

        def rows_step(c, carry):
            these = chunk_rows(c)
            put(c, these, dot(part[these, :], wt[lax.rem(j, 4)]))
            return carry
        lax.fori_loop(0, N_CHUNK, rows_step, 0)
        start_w(j + 4)

    def v_step(j, carry):
        def put(c, these, acc):
            r['values'][aligned(base + c * chunk, chunk), cols(j)] = acc.astype(BF16)
        head_tile(j, put)
        return carry

    def k_step(j, carry):
        def put(c, these, acc):
            r['keys'][aligned(base + c * chunk, chunk), cols(j)] = rope(acc, these, 1.0 + qk_ref[2 * layer + 1:2 * layer + 2, :]).astype(BF16)
        head_tile(j + n_kv, put)
        return carry

    def q_step(j, carry):
        def put(c, these, acc):
            qo[these, cols(j)] = (rope(acc, these, 1.0 + qk_ref[2 * layer:2 * layer + 1, :]).astype(BF16).astype(F32) * (HEAD ** -0.5)).astype(BF16)
        head_tile(j + 2 * n_kv, put)
        return carry
    lax.fori_loop(0, n_kv, v_step, 0)
    lax.fori_loop(0, n_kv, k_step, 0)
    new_kv = [r[buf].at[pl.ds(base, rows)] for buf in ('keys', 'values')]
    kv_out = [pltpu.make_async_copy(src, r[dst], r['kv_sem'].at[i]) for i, (src, dst) in enumerate(zip(new_kv, ('k_new', 'v_new')))]
    if first_layer:
        sends = [to_cp(src, r[buf].at[pl.ds(0, rows)], 'n', i, right) for i, (src, buf) in enumerate(zip(new_kv, ('keys', 'values')))]

        @pl.when(jnp.logical_not(is_last))
        def _():
            for copy in sends:
                copy.start()
    else:
        alls = ('kn_all', 'vn_all')
        n_across = [to_cp(src, r[dst].at[cp], 'n', i, across) for i, (src, dst) in enumerate(zip(new_kv, alls))]
        n_near = [to_cp(src, r[dst].at[cp], 'n', 2 + i, near) for i, (src, dst) in enumerate(zip(new_kv, alls))]
        n_relay = [to_cp(r[dst].at[across], r[dst].at[across], 'n', 4 + i, near) for i, dst in enumerate(alls)]
        n_own = [pltpu.make_async_copy(src, r[dst].at[cp], r['own_sem'].at[i]) for i, (src, dst) in enumerate(zip(new_kv, alls))]
        for copy in n_across + n_near + n_own:
            copy.start()
    for copy in kv_out:
        copy.start()
    for t in range(n_dim):
        wo_copy(t).start()
    if not first_layer:
        x_copy = pltpu.make_async_copy(x_hbm, xv, r['x_sem'].at[0])
        x_copy.start()
    lax.fori_loop(0, n_q, q_step, 0)
    for i in range(2):
        for copy in gu_copies(jnp.int32(i)):
            copy.start()
        dn_copy(jnp.int32(i)).start()

    def to_tp(src, dst, send_sem, recv_sem, peer):
        return pltpu.make_async_remote_copy(src_ref=src, dst_ref=dst, send_sem=send_sem, recv_sem=recv_sem, device_id={'tp': peer}, device_id_type=MESH)

    def hop1(n):
        return to_tp(part.at[rows_of(n)], tot.at[rows_of(n)], r['s1'].at[n], r['s1'].at[n], mate)

    def hop2(n):
        return to_tp(part.at[rows_of(n)], recv2.at[lax.rem(n, RECV_SLOTS)], r['s2s'].at[n], r['s2r'].at[n], middle)

    def hop3(n):
        return to_tp(tot.at[rows_of(n)], tot.at[rows_of(n)], r['s3'].at[n], r['s3'].at[n], mate)

    def out_copies(n):
        made = [pltpu.make_async_copy(xv.at[rows_of(n)], r['x_out'].at[rows_of(n)], r['out_sem'].at[0, lax.rem(n, per)])]
        if first_layer:
            made.append(pltpu.make_async_copy(part.at[rows_of(n)], r['h_out'].at[rows_of(n)], r['out_sem'].at[1, lax.rem(n, per)]))
        return made

    def send_chunk(first):
        @pl.when(outer)
        def _():
            for i in range(N_SUB):
                hop1(first + i).start()

    def normalize(n):
        start = lax.rem(n, per) * sub
        step = min(16, sub)

        def update(these, row):
            value = (xv[these, :].astype(F32) + unit_rms(tot[these, :].astype(F32)) * (1.0 + g_ref[row:row + 1, :])).astype(BF16)
            xv[these, :] = value
            return value.astype(F32)

        @pl.when(n < per)
        def _():
            def body(i, carry):
                these = aligned(start + i * step, step)
                value = update(these, 4 * layer + 1)
                part[these, :] = (unit_rms(value) * (1.0 + g_ref[4 * layer + 2:4 * layer + 3, :])).astype(BF16)
                return carry
            lax.fori_loop(0, sub // step, body, 0)

        @pl.when(n >= per)
        def _():
            def body(i, carry):
                these = aligned(start + i * step, step)
                value = update(these, 4 * layer + 3)
                if first_layer:
                    part[these, :] = (unit_rms(value) * (1.0 + g_ref[4:5, :])).astype(BF16)
                return carry
            lax.fori_loop(0, sub // step, body, 0)
            for copy in out_copies(n):
                copy.start()

    def event(tick):
        n, k, m = tick, tick - 1, tick - 2

        @pl.when(inner)
        def _():
            @pl.when((n >= 0) & (n < n_ev))
            def _():
                hop1(n).wait_recv()
                these = rows_of(n)
                part[these, :] = (part[these, :].astype(F32) + tot[these, :].astype(F32)).astype(BF16)

                @pl.when(n >= RECV_SLOTS)
                def _():
                    pl.semaphore_wait(r['credit'], 1)

            @pl.when((k >= 0) & (k < n_ev))
            def _():
                hop2(k).wait_recv()
                hop2(k).wait_send()
                these = rows_of(k)
                tot[these, :] = (part[these, :].astype(F32) + recv2[lax.rem(k, RECV_SLOTS)].astype(F32)).astype(BF16)

                @pl.when(k < n_ev - RECV_SLOTS)
                def _():
                    pl.semaphore_signal(r['credit'], inc=1, device_id={'tp': middle}, device_id_type=MESH)

            @pl.when((n >= 0) & (n < n_ev))
            def _():
                hop2(n).start()

            @pl.when((k >= 1) & (k < n_ev))
            def _():
                hop3(k - 1).wait_send()

        @pl.when(outer & (m >= 0) & (m < n_ev))
        def _():
            hop1(m).wait_send()
            hop3(m).wait_recv()
        late = jnp.where(inner, k, m)

        @pl.when((late >= 0) & (late < n_ev))
        def _():
            normalize(late)

            @pl.when(inner)
            def _():
                hop3(late).start()

    def event_loop(low, high):
        def body(tick, carry):
            event(tick)
            return carry
        lax.fori_loop(low, high, body, 0)

    def project_chunk(c):
        these = chunk_rows(c)

        def tile(t, carry):
            @pl.when(c == 0)
            def _():
                wo_copy(t).wait()
            part[these, cols(t)] = dot(qo[these, :], wo_v[:, cols(t)]).astype(BF16)
            return carry
        lax.fori_loop(0, n_dim, tile, 0)
        send_chunk(c * N_SUB)

    if first_layer:
        @pl.when(is_first)
        def _():
            for copy in old_copies:
                copy.wait()

        @pl.when(jnp.logical_not(is_first))
        def _():
            for copy in sends:
                copy.wait_recv()
        caches = ('k_own', 'v_own')
        alls = ('k_all', 'v_all')
        c_across = [to_cp(r[src], r[dst].at[cp], 'g', i, across) for i, (src, dst) in enumerate(zip(caches, alls))]
        c_near = [to_cp(r[src], r[dst].at[cp], 'g', 2 + i, near) for i, (src, dst) in enumerate(zip(caches, alls))]
        c_relay = [to_cp(r[dst].at[across], r[dst].at[across], 'g', 4 + i, near) for i, dst in enumerate(alls)]

        @pl.when(jnp.logical_not(is_last))
        def _():
            for copy in sends:
                copy.wait_send()
        for copy in c_across + c_near:
            copy.start()
        span = rows + chunk

        def window_chunk(c, carry):
            these = chunk_rows(c)
            seen_keys = pl.ds(pl.multiple_of(c * chunk, chunk), span)
            row_id = lax.broadcasted_iota(jnp.int32, (chunk, span), 0)
            col_id = lax.broadcasted_iota(jnp.int32, (chunk, span), 1)
            seen = (col_id > row_id) & (col_id <= row_id + rows)
            for head in range(n_kv):
                key = r['keys'][seen_keys, head * HEAD:(head + 1) * HEAD]
                value = r['values'][seen_keys, head * HEAD:(head + 1) * HEAD]
                for g in range(groups):
                    these_cols = slice((head * groups + g) * HEAD, (head * groups + g + 1) * HEAD)
                    scores = jnp.where(seen, dot_t(qo[these, these_cols], key), NEG_BIG)
                    top = jnp.max(scores, axis=-1, keepdims=True)
                    prob = jnp.exp(scores - top)
                    total = jnp.sum(prob, axis=-1, keepdims=True)
                    qo[these, these_cols] = (dot(prob.astype(BF16), value) / total).astype(BF16)
            project_chunk(c)
            return carry
        lax.fori_loop(0, N_CHUNK, window_chunk, 0)
        next_tick = 6
        event_loop(0, next_tick)
    else:
        block = rows
        shard = r['k_own'].shape[0]
        per_shard = shard // block
        n_cache = size * per_shard
        n_mask = -(-(shard // 2) // block)
        n_full = n_cache - n_mask
        n_blocks = n_cache + cp + 1
        first_pos = r['first_pos'][0]
        stack = groups * chunk
        step = min(256, stack)
        scores_refs = (r['s_even'], r['s_odd'])

        def fetch(b, own, every, new, dst, sem, op):
            cache_id = jnp.where(b < n_mask, n_full + b, b - n_mask)
            s = cache_id // per_shard
            where = aligned(lax.rem(cache_id, per_shard) * block, block)

            @pl.when((b < n_cache) & (s == cp))
            def _():
                getattr(pltpu.make_async_copy(own.at[where], dst, sem), op)()

            @pl.when((b < n_cache) & (s != cp))
            def _():
                getattr(pltpu.make_async_copy(every.at[jnp.clip(s, 0, size - 1), where], dst, sem), op)()

            @pl.when(b >= n_cache)
            def _():
                getattr(pltpu.make_async_copy(new.at[jnp.clip(b - n_cache, 0, size - 1)], dst, sem), op)()

        def fetch_k(i, b, op):
            slot = lax.rem(i, 3)
            fetch(b, r['k_own'], r['k_all'], r['kn_all'], r['kb'].at[slot], r['kb_sem'].at[slot], op)

        def fetch_v(i, b, op):
            slot = lax.rem(i, 2)
            fetch(b, r['v_own'], r['v_all'], r['vn_all'], r['vb'].at[slot], r['vb_sem'].at[slot], op)

        def arrived():
            for copy in n_near + n_across:
                copy.wait()
            for copy in n_relay:
                copy.start()
            for copy in n_relay:
                copy.wait()
            for copy in n_own:
                copy.wait()

        def raw_scores(c, head, slot):
            query = jnp.concatenate([qo[chunk_rows(c), (head * groups + g) * HEAD:(head * groups + g + 1) * HEAD] for g in range(groups)], axis=0)
            scores_refs[head][...] = dot_t(query, r['kb'][slot, :, head * HEAD:(head + 1) * HEAD])

        def absorb(head, slot, seen_of):
            value = r['vb'][slot, :, head * HEAD:(head + 1) * HEAD]
            for low in range(0, stack, step):
                these = slice(low, low + step)
                scores = scores_refs[head][these, :]
                if seen_of is not None:
                    scores = jnp.where(seen_of(low, scores.shape), scores, NEG_BIG)
                state = slice(head * stack + low, head * stack + low + step)
                old = r['top'][state, :]
                new = jnp.maximum(old, jnp.max(scores, axis=-1, keepdims=True))
                decay = jnp.exp(old - new)
                prob = jnp.exp(scores - jnp.concatenate([new] * (block // 128), axis=1))
                lanes = prob[:, :128]
                for i in range(1, block // 128):
                    lanes = lanes + prob[:, i * 128:(i + 1) * 128]
                r['sums'][state, :] = r['sums'][state, :] * decay + lanes
                r['top'][state, :] = new
                r['acc'][head, these, :] = r['acc'][head, these, :] * jnp.concatenate([decay] * (HEAD // 128), axis=1) + dot(prob.astype(BF16), value)

        marks = [n_full * k // 9 for k in (2, 5, 8)]

        def attend_chunk(c, carry):
            start = c * n_blocks
            r['top'][...] = jnp.full(r['top'].shape, NEG_BIG, F32)
            r['sums'][...] = jnp.zeros(r['sums'].shape, F32)
            r['acc'][...] = jnp.zeros(r['acc'].shape, F32)

            @pl.when(c == 0)
            def _():
                fetch_k(0, 0, 'start')
                fetch_v(0, 0, 'start')
                fetch_k(1, 1, 'start')
                fetch_k(0, 0, 'wait')
            raw_scores(c, 0, lax.rem(start, 3))

            def block_step(seen_kind, b, carry):
                i = start + b
                fetch_v(i, b, 'wait')
                last = b == n_blocks - 1
                more = jnp.logical_not(last & (c == N_CHUNK - 1))

                @pl.when((c == 0) & (b + 2 == n_cache))
                def _():
                    arrived()

                @pl.when(more)
                def _():
                    fetch_k(i + 1, jnp.where(last, 0, b + 1), 'wait')
                    fetch_v(i + 1, jnp.where(last, 0, b + 1), 'start')

                @pl.when(jnp.logical_not((b >= n_blocks - 2) & (c == N_CHUNK - 1)))
                def _():
                    fetch_k(i + 2, jnp.where(b >= n_blocks - 2, b + 2 - n_blocks, b + 2), 'start')
                slot, later, v_slot = lax.rem(i, 3), lax.rem(i + 1, 3), lax.rem(i, 2)

                def seen_of(low, shape):
                    col_id = lax.broadcasted_iota(jnp.int32, shape, 1)
                    if seen_kind == 'cache':
                        return col_id < first_pos - (n_full + b) * block
                    row_id = lax.rem(low, chunk) + lax.rem(lax.broadcasted_iota(jnp.int32, shape, 0), chunk)
                    return col_id - row_id <= c * chunk
                seen = None if seen_kind is None else seen_of
                raw_scores(c, 1, slot)
                absorb(0, v_slot, seen)
                raw_scores(c, 0, later)
                absorb(1, v_slot, seen)
                if seen_kind is None:
                    at = b - n_mask
                    hit = (at == marks[0]) | (at == marks[1]) | (at == marks[2])

                    @pl.when(hit & (c > 0))
                    def _():
                        event((c - 1) * N_SUB + (at > marks[0]).astype(jnp.int32) + (at > marks[1]).astype(jnp.int32))
                return carry
            lax.fori_loop(0, n_mask, functools.partial(block_step, 'cache'), 0)
            lax.fori_loop(n_mask, n_cache + cp, functools.partial(block_step, None), 0)
            lax.fori_loop(n_cache + cp, n_blocks, functools.partial(block_step, 'own'), 0)
            these = chunk_rows(c)
            for head in range(n_kv):
                total = jnp.sum(r['sums'][head * stack:(head + 1) * stack, :], axis=-1, keepdims=True)
                result = (r['acc'][head] / total).astype(BF16)
                for g in range(groups):
                    qo[these, (head * groups + g) * HEAD:(head * groups + g + 1) * HEAD] = result[g * chunk:(g + 1) * chunk]
            project_chunk(c)

            @pl.when(c > 0)
            def _():
                event((c - 1) * N_SUB + 3)
            return carry
        x_copy.wait()
        lax.fori_loop(0, N_CHUNK, attend_chunk, 0)
        next_tick = (N_CHUNK - 1) * N_SUB

    tasks = n_ff + n_dim
    ffn_marks = spread(N_SUB, [2] * n_ff + [1] * n_dim)

    def ffn_chunk(c, carry):
        these = chunk_rows(c)

        def task(t, carry):
            @pl.when(t < n_ff)
            def _():
                i = c * n_ff + t
                for copy in gu_copies(i):
                    copy.wait()
                slot = lax.rem(i, 2) * 2
                lhs = part[these, :]
                gate = dot(lhs, wt[slot])
                up = dot(lhs, wt[slot + 1])
                hact[:, cols(t)] = (jax.nn.gelu(gate, approximate=True) * up).astype(BF16)

                @pl.when(i + 2 < N_CHUNK * n_ff)
                def _():
                    for copy in gu_copies(i + 2):
                        copy.start()

            @pl.when(t >= n_ff)
            def _():
                i = c * n_dim + t - n_ff
                dn_copy(i).wait()
                part[these, cols(t - n_ff)] = dot(hact[...], dn[lax.rem(i, 2)]).astype(BF16)

                @pl.when(i + 2 < N_CHUNK * n_dim)
                def _():
                    dn_copy(i + 2).start()
            hit = t == ffn_marks[0]
            which = jnp.int32(0)
            for mark in ffn_marks[1:]:
                which = which + (t >= mark).astype(jnp.int32)
                hit = hit | (t == mark)

            @pl.when(hit)
            def _():
                event(next_tick + c * N_SUB + which)
            return carry
        lax.fori_loop(0, tasks, task, 0)
        send_chunk(per + c * N_SUB)
        return carry
    lax.fori_loop(0, N_CHUNK, ffn_chunk, 0)
    drain = next_tick + N_CHUNK * N_SUB
    if first_layer:
        event_loop(drain, n_ev - 3)
        for copy in c_across:
            copy.wait()
        for copy in c_relay:
            copy.start()
        event_loop(n_ev - 3, n_ev + 2)
    else:
        event_loop(drain, n_ev + 2)

    @pl.when(inner)
    def _():
        hop3(n_ev - 1).wait_send()

    def finish(m, carry):
        for copy in out_copies(m):
            copy.wait()
        return carry
    lax.fori_loop(0, per, finish, 0)
    for copy in kv_out:
        copy.wait()
    if first_layer:
        for copy in c_near + c_relay:
            copy.wait()


def run_layer(layer, ins, collective_id):
    rows, dim = ins['x'].shape
    q_cols, kv_cols, ff = ins['w_query'].shape[2], ins['w_key'].shape[2], ins['w_gate'].shape[2]
    shard = ins['k_own'].shape[0]
    first_layer = layer == 0
    chunk = rows // N_CHUNK
    sub = chunk // N_SUB
    n_ev = 2 * N_CHUNK * N_SUB
    groups, n_kv = q_cols // kv_cols, kv_cols // HEAD
    stack = groups * chunk
    in_vmem = ('gains', 'qk_gains', 'cos', 'sin') if first_layer else ('gains', 'qk_gains')

    def spec(name):
        if name == 'first_pos':
            return pl.BlockSpec(memory_space=pltpu.SMEM)
        return pl.BlockSpec(memory_space=pltpu.VMEM if name in in_vmem else pl.ANY)
    array = jax.ShapeDtypeStruct
    outs = {'x_out': array((rows, dim), BF16), 'k_new': array((rows, kv_cols), BF16), 'v_new': array((rows, kv_cols), BF16)}
    dma = pltpu.SemaphoreType.DMA
    scratch = {
        'part': pltpu.VMEM((rows, dim), BF16),
        'tot': pltpu.VMEM((rows, dim), BF16),
        'xv': pltpu.VMEM((rows, dim), BF16),
        'wt': pltpu.VMEM((4, dim, TILE), BF16),
        'dn': pltpu.VMEM((2, ff, TILE), BF16),
        'wo_v': pltpu.VMEM((q_cols, dim), BF16),
        'qo': pltpu.VMEM((rows, q_cols), BF16),
        'hact': pltpu.VMEM((chunk, ff), BF16),
        'recv2': pltpu.VMEM((RECV_SLOTS, sub, dim), BF16),
        'w_sem': dma((4,)), 'dn_sem': dma((2,)), 'wo_sem': dma((dim // TILE,)), 'h_sem': dma((N_CHUNK,)),
        'kv_sem': dma((2,)), 'n_s': dma((6,)), 'n_r': dma((6,)),
        's1': dma((n_ev,)), 's2s': dma((n_ev,)), 's2r': dma((n_ev,)), 's3': dma((n_ev,)),
        'credit': pltpu.SemaphoreType.REGULAR, 'out_sem': dma((2, n_ev // 2)),
    }
    key_rows = 2 * rows if first_layer else rows
    scratch |= {'keys': pltpu.VMEM((key_rows, kv_cols), BF16), 'values': pltpu.VMEM((key_rows, kv_cols), BF16)}
    if first_layer:
        outs |= {'h_out': array((rows, dim), BF16), 'k_all': array((4, shard, kv_cols), BF16), 'v_all': array((4, shard, kv_cols), BF16)}
        scratch |= {'old_sem': dma((2,)), 'g_s': dma((6,)), 'g_r': dma((6,))}
    else:
        outs |= {'kn_all': array((4, rows, kv_cols), BF16), 'vn_all': array((4, rows, kv_cols), BF16)}
        scratch |= {
            'kb': pltpu.VMEM((3, rows, kv_cols), BF16),
            'vb': pltpu.VMEM((2, rows, kv_cols), BF16),
            's_even': pltpu.VMEM((stack, rows), F32),
            's_odd': pltpu.VMEM((stack, rows), F32),
            'top': pltpu.VMEM((n_kv * stack, 128), F32),
            'sums': pltpu.VMEM((n_kv * stack, 128), F32),
            'acc': pltpu.VMEM((n_kv, stack, HEAD), F32),
            'kb_sem': dma((3,)), 'vb_sem': dma((2,)), 'own_sem': dma((2,)), 'x_sem': dma((1,)),
        }
    names = tuple(ins) + tuple(outs) + tuple(scratch)
    made = pl.pallas_call(
        functools.partial(layer_kernel, layer, names),
        out_shape=tuple(outs.values()),
        in_specs=[spec(name) for name in ins],
        out_specs=tuple(pl.BlockSpec(memory_space=pl.ANY) for _ in outs),
        scratch_shapes=list(scratch.values()),
        compiler_params=pltpu.CompilerParams(collective_id=collective_id, has_side_effects=True, vmem_limit_bytes=VMEM_LIMIT),
        name='layer_%d' % layer,
    )(*ins.values())
    return dict(zip(outs, made))


def solution(mesh):
    row_spec = P(('dp', 'cp'), None)
    cache_spec = P(('dp', 'cp'), 'tp', None)
    window_spec = P('dp', 'tp', None)
    col_spec = P(None, None, 'tp')
    row_split = P(None, 'tp', None)
    replicated = P()

    def device_step(hidden, start_pos, k_local, v_local, k_global, v_global, w_query, w_key, w_value, w_out, w_gate, w_up, w_down, norm_gain, qk_gain):
        first_pos = start_pos[0]
        cp_index = lax.axis_index('cp')
        rows, dim = hidden.shape
        window = k_local.shape[0]
        flat = lambda a: a.reshape(a.shape[0], -1)
        positions = first_pos + cp_index * rows + jnp.arange(rows)
        gains = jnp.concatenate([norm_gain.reshape(8, dim), jnp.zeros((8, dim), F32)], axis=0)
        qk_gains = jnp.concatenate([qk_gain.reshape(4, HEAD), jnp.zeros((4, HEAD), F32)], axis=0)
        turn = jnp.remainder(first_pos, window)
        rolled = [lax.dynamic_slice_in_dim(jnp.concatenate([flat(a), flat(a)], axis=0), turn, window, axis=0) for a in (k_local, v_local)]
        cache = (flat(k_global), flat(v_global))
        weights = {'w_query': w_query, 'w_key': w_key, 'w_value': w_value, 'w_out': w_out, 'w_gate': w_gate, 'w_up': w_up, 'w_down': w_down, 'k_own': cache[0], 'v_own': cache[1]}
        cos, sin = rope_tables(positions, LOCAL_BASE, 1.0)
        one = run_layer(0, {'x': hidden, 'gains': gains, 'qk_gains': qk_gains, 'cos': cos, 'sin': sin, 'k_old': rolled[0], 'v_old': rolled[1], **weights}, 0)
        cos, sin = rope_tables(positions, GLOBAL_BASE, GLOBAL_DIV)
        two = run_layer(1, {'first_pos': start_pos, 'x': one['x_out'], 'h': one['h_out'], 'gains': gains, 'qk_gains': qk_gains, 'cos': cos, 'sin': sin, 'k_all': one['k_all'], 'v_all': one['v_all'], **weights}, 1)
        shaped = lambda a: a.reshape(rows, -1, HEAD)
        return two['x_out'], shaped(one['k_new']), shaped(one['v_new']), shaped(two['k_new']), shaped(two['v_new'])

    return jax.shard_map(device_step, mesh=mesh, in_specs=(row_spec, P('dp'), window_spec, window_spec, cache_spec, cache_spec, col_spec, col_spec, col_spec, row_split, col_spec, col_spec, row_split, replicated, replicated), out_specs=(row_spec, cache_spec, cache_spec, cache_spec, cache_spec), check_vma=False)
```

time: 2430 us -> 1050 us (0.43)
  waiting for transfers between devices: 1270 us -> 0 us
  Pallas kernels: 0 us -> 1010 us
  matrix products: 767 us -> 0 us
  other arithmetic: 260 us -> 10.1 us
  local copies, waits for them, and re-layouts: 88 us -> 28 us
    psum x4 -> x0, waiting for transfers between devices: 1070 us -> none  [the longest x2 549 us: finish(): lax.psum(jnp.dot(attn_out.reshape(row_count, -1), w_out, preferred_elemen...]
    pallas_call x0 -> x2, Pallas kernels: none -> 1010 us  [run_layer(): pl.pallas_call(functools.partial(layer_kernel, layer, names), out_shape=t...]
    dot_general x31 -> x0, matrix products: 740 us -> none  [the longest x4 155 us: partial_block(): jnp.einsum('qkgt,tkd->qkgd', cache_exp.astype(jnp.bfloat16), cache_v, pre...]
    reduce_sum x18 -> x0, other arithmetic: 210 us -> none  [the longest x8 156 us: partial_block(): row_sum = cache_exp.sum(axis=-1) + own_exp.sum(axis=-1)]
    all_to_all x1 -> x0, waiting for transfers between devices: 181 us -> none  [spread_attention(): got_out = lax.all_to_all(part_out, 'cp', 0, 0, tiled=True)]
    dot_general x6 -> x0, local copies, waits for them, and re-layouts: 43.5 us -> none  [the longest x3 27.2 us: project(): jnp.dot(normed, w_query, preferred_element_type=jnp.float32)]
    sub x1 -> x0, matrix products: 27.8 us -> none  [window_attention(): attn_prob = jax.nn.softmax(scores, axis=-1).astype(jnp.bfloat16)]
  transfers between devices with their start and end apart: 8 -> 0, of which waited for: 6 -> 0; matrix products, arithmetic and copies ran while one was open for 6% -> 0% of each run, Pallas kernels for 0% -> 0%
where the time goes in v2:
time: 1050 us
  Pallas kernels  1010 us (96%)
  local copies, waits for them, and re-layouts  28 us (3%)
    pallas_call x2, Pallas kernels, run_layer(): pl.pallas_call(functools.partial(layer_kernel, layer, names), out_shape=t...  1010 us

profile of v2, /device:TPU:4, one launch (start us, length us, event | category | flops | bytes accessed | tf_op | source)
XLA Modules:
  0.0 1045.6 jit_solution(10678137339935269630)
XLA Ops:
  1.3 0.7 reshape.60
  2.0 0.6 concatenate.13.refs_2_.refs_4_
  2.6 0.9 reshape.59
  3.6 0.0 copy-start
  3.6 0.7 concatenate.12.refs_1_.refs_3_
  4.3 3.0 multiply_sine_fusion.1
  7.3 3.1 multiply_sine_fusion
  10.4 1.4 copy.20
  11.9 1.4 copy.21
  13.3 0.0 slice-start
  13.3 4.0 fusion
  17.3 0.0 copy-done
  17.3 0.0 slice-start.1
  17.3 3.8 copy.22
  21.1 0.0 slice-done
  21.1 0.0 slice-done.1
  21.1 3.8 copy.23
  24.9 472.4 %layer_0.1 = (bf16[1024,3840]{1,0:T(8,128)(2,1)}, bf16[1024,512]{1,0:T(8,128)(2,1)}, bf16[1024,512]{1,0:T(8,128)(2,1)}, bf16[1024,3840]{1,0:T(8,128)(2,1)}, bf16...) custom-call(bf16[1024,3840]{1,0:T(8,128)(2,1)} %refs_0_.2, f32[16,3840]{1,0:T(8,128)} %concatenate.12.refs_1_.refs_3_, ...), custom_call_target="tpu_custom_call" | custom-call | tf_op jit(solution)/shard_map/layer_0/pallas_call | solution.py:669
  497.3 533.7 %layer_1.1 = (bf16[1024,3840]{1,0:T(8,128)(2,1)}, bf16[1024,512]{1,0:T(8,128)(2,1)}, bf16[1024,512]{1,0:T(8,128)(2,1)}, bf16[4,1024,512]{2,1,0:T(8,128)(2,1)}, bf16[4,1024,512]{2,1,0:T(8,128)(2,1)}) custom-call(s32[1]{0:T(128)} %copy.25.refs_0_, bf16[1024,3840]{1,0:T(8,128)(2,1)} %get-tuple-element.14.refs_1_, bf16[1024,3840]{1,0:T(8,128)(2,1)} %get-tuple-element.15.refs_2_, ...), custom_call_target="tpu_custom_call" | custom-call | tf_op jit(solution)/shard_map/layer_1/pallas_call | solution.py:669
  1031.1 0.0 copy-start.1
  1031.1 2.2 reshape.67
  1033.3 2.1 reshape.68
  1035.5 2.1 reshape.65
  1037.6 0.0 copy-done.1
  1037.6 1.1 reshape.66
  1038.7 7.0 copy.26
  (5 shorter events, 0.0 us)
Async XLA Ops:
  3.6 13.7 %copy-start = (bf16[6144,2,256]{2,1,0:T(2,128)(2,1)S(1)}, bf16[6144,2,256]{2,1,0:T(2,128)(2,1)}, u32[]{:S(2)}) copy-start(bf16[6144,2,256]{2,1,0:T(2,128)(2,1)} %param.19) | copy-start | bytes 18874372
  13.3 7.8 slice-start
  17.3 3.8 slice-start.1
  1031.1 6.5 copy-start.1

commit v3 on v0

v3 whole, which is shorter than its diff:
```python
import functools
import types

import jax
import jax.numpy as jnp
from jax import lax
from jax.experimental import pallas as pl
from jax.experimental.pallas import tpu as pltpu
from jax.sharding import PartitionSpec as P

NORM_EPS = 1e-6
LOCAL_BASE = 10000.0
GLOBAL_BASE = 1000000.0
GLOBAL_DIV = 8.0
NEG_BIG = -1e30
HEAD = 256
TILE = 256
VMEM_LIMIT = 67_000_000
MESH = pl.DeviceIdType.MESH
F32 = jnp.float32
BF16 = jnp.bfloat16


def dot(a, b):
    return jnp.dot(a, b, preferred_element_type=F32)


def dot_t(a, b):
    return lax.dot_general(a, b, (((1,), (1,)), ((), ())), preferred_element_type=F32)


def unit_rms(values):
    return values * lax.rsqrt(jnp.mean(values * values, axis=-1, keepdims=True) + NORM_EPS)


def rope_tables(first, rows, rope_base, divisor):
    half, step = HEAD // 2, 32
    inv_freq = 1.0 / (rope_base ** (jnp.arange(0, 2 * half, 2, dtype=F32) / (2 * half)))
    fine = (jnp.arange(step).astype(F32) / divisor)[:, None] * inv_freq[None, :]
    coarse = ((first + jnp.arange(0, rows, step)).astype(F32) / divisor)[:, None] * inv_freq[None, :]
    cos_f, sin_f, cos_c, sin_c = lax.optimization_barrier((jnp.cos(fine)[None], jnp.sin(fine)[None], jnp.cos(coarse)[:, None], jnp.sin(coarse)[:, None]))
    return (cos_c * cos_f - sin_c * sin_f).reshape(rows, half), (sin_c * cos_f + cos_c * sin_f).reshape(rows, half)


def enter(peers):
    for peer in peers:
        pl.semaphore_signal(pltpu.get_barrier_semaphore(), inc=1, device_id=peer, device_id_type=MESH)


def entered(peers):
    pl.semaphore_wait(pltpu.get_barrier_semaphore(), len(peers))


N_CHUNK = 4
N_SUB = 4
RECV_SLOTS = 4
LAG = 2
W_SLOTS = 6
D_SLOTS = 3
O_TILES = 3


def begin(copy):
    copy.start()


def end(copy):
    copy.wait()


def spread(count, weights):
    total, seen, marks = sum(weights), 0, []
    for i, weight in enumerate(weights):
        seen += weight
        if seen * count >= total * (len(marks) + 1):
            marks.append(i)
    return marks


def layers_kernel(names, *refs):
    r = types.SimpleNamespace(**dict(zip(names, refs)))
    x_hbm, g_ref, qk_ref = r.x, r.gains, r.qk_gains
    part, tot, xv, wt, dn, qo, hact, recv2 = r.part, r.tot, r.xv, r.wt, r.dn, r.qo, r.hact, r.recv2
    keys, values, top, sums, acc_ref = r.keys, r.values, r.top, r.sums, r.acc
    rows, dim = x_hbm.shape
    ff = r.w_gate.shape[2]
    kv_cols = r.w_key.shape[2]
    q_cols = r.w_query.shape[2]
    n_kv, n_q = kv_cols // HEAD, q_cols // HEAD
    groups = n_q // n_kv
    chunk = rows // N_CHUNK
    sub = chunk // N_SUB
    per = N_CHUNK * N_SUB
    n_ev = 2 * per
    n_tick = n_ev + LAG
    n_dim, n_ff = dim // TILE, ff // TILE
    tp, cp, size = lax.axis_index('tp'), lax.axis_index('cp'), lax.axis_size('cp')
    outer = (tp == 0) | (tp == 3)
    inner = jnp.logical_not(outer)
    mate = tp + 1 - 2 * lax.rem(tp, 2)
    middle = 3 - tp
    near = cp + 1 - 2 * lax.rem(cp, 2)
    across = lax.rem(cp + 2, size)
    far = lax.rem(near + 2, size)
    right = lax.rem(cp + 1, size)
    is_first, is_last = cp == 0, cp == size - 1

    def aligned(start, length):
        return pl.ds(pl.multiple_of(start, length), length)

    def cols(t):
        return aligned(t * TILE, TILE)

    def row_start(c):
        return (N_CHUNK - 1 - c) * chunk

    def chunk_rows(c):
        return aligned(row_start(c), chunk)

    def sub_start(n):
        m = lax.rem(n, per)
        return row_start(m // N_SUB) + lax.rem(m, N_SUB) * sub

    def rows_of(n):
        return aligned(sub_start(n), sub)

    n_tile = 2 * n_kv + n_q

    def start_w(layer, j):
        for low, high, w_hbm in ((0, n_kv, r.w_value), (n_kv, 2 * n_kv, r.w_key), (2 * n_kv, n_tile, r.w_query)):
            @pl.when((j >= low) & (j < high))
            def _():
                slot = lax.rem(j, W_SLOTS)
                pltpu.make_async_copy(w_hbm.at[layer, :, cols(jnp.clip(j - low, 0, high - low - 1))], wt.at[slot], r.w_sem.at[slot]).start()

    def wait_w(layer, j):
        slot = lax.rem(j, W_SLOTS)
        pltpu.make_async_copy(r.w_value.at[layer, :, cols(0)], wt.at[slot], r.w_sem.at[slot]).wait()

    per_slot = dim // q_cols
    places = W_SLOTS * per_slot

    def wo_place(k):
        place = lax.rem(k, places)
        return wt.at[place // per_slot, aligned(lax.rem(place, per_slot) * q_cols, q_cols)], r.wo_sem.at[place]

    def wo_copy(layer, k):
        dst, sem = wo_place(k)
        return pltpu.make_async_copy(r.w_out.at[layer, :, cols(lax.rem(k, n_dim))], dst, sem)

    def start_wo(layer):
        def body(k, carry):
            wo_copy(layer, k).start()
            return carry
        lax.fori_loop(0, places, body, 0)

    def gu_copies(layer, i):
        slot, t = lax.rem(i, W_SLOTS // 2) * 2, lax.rem(i, n_ff)
        return [pltpu.make_async_copy(w.at[layer, :, cols(t)], wt.at[slot + k], r.w_sem.at[slot + k]) for k, w in enumerate((r.w_gate, r.w_up))]

    def dn_copy(layer, i):
        slot = lax.rem(i, D_SLOTS)
        return pltpu.make_async_copy(r.w_down.at[layer, :, cols(lax.rem(i, n_dim))], dn.at[slot], r.dn_sem.at[slot])

    def start_gu(layer):
        for i in range(W_SLOTS // 2):
            for copy in gu_copies(layer, jnp.int32(i)):
                copy.start()

    def start_dn(layer):
        for i in range(D_SLOTS):
            dn_copy(layer, jnp.int32(i)).start()

    peers = [{'tp': mate}, {'tp': middle}, {'cp': near}, {'cp': across}, {'cp': far}]
    enter(peers)
    x_copies = [pltpu.make_async_copy(x_hbm.at[pl.ds(i * chunk, chunk)], xv.at[pl.ds(i * chunk, chunk)], r.x_sem.at[i]) for i in range(N_CHUNK)]
    x_copies[0].start()
    start_w(0, jnp.int32(0))
    for copy in x_copies[1:]:
        copy.start()
    for j in range(1, W_SLOTS):
        start_w(0, jnp.int32(j))
    half = n_kv * groups * chunk
    cos_ref, sin_ref = top.at[pl.ds(0, half)], sums.at[pl.ds(0, half)]
    t_copies = [pltpu.make_async_copy(table, dst, r.t_sem.at[i]) for i, (table, dst) in enumerate(((r.cos_local, cos_ref), (r.sin_local, sin_ref)))]
    for copy in t_copies:
        copy.start()
    start_dn(0)
    old_copies = [pltpu.make_async_copy(old, buf.at[pl.ds(0, rows)], r.old_sem.at[i]) for i, (old, buf) in enumerate(((r.k_old, keys), (r.v_old, values)))]

    @pl.when(is_first)
    def _():
        for copy in old_copies:
            copy.start()

    def to_cp(src, dst, sems, i, peer):
        return pltpu.make_async_remote_copy(src_ref=src, dst_ref=dst, send_sem=sems[0].at[i], recv_sem=sems[1].at[i], device_id={'cp': peer}, device_id_type=MESH)

    block = rows
    shard = r.k_own.shape[0]
    per_shard = shard // block
    own_names = ((r.k_own, r.k_all), (r.v_own, r.v_all))
    c_near = [to_cp(src, dst.at[cp], (r.c_near_s, r.c_near_r), i, near) for i, (src, dst) in enumerate(own_names)]

    def c_across(i):
        where = aligned(i * block, block)
        return [to_cp(src.at[where], dst.at[cp, where], (r.c_across_s, r.c_across_r), 2 * i + k, across) for k, (src, dst) in enumerate(own_names)]

    def c_relay(i):
        where = aligned(i * block, block)
        return [to_cp(dst.at[across, where], dst.at[across, where], (r.c_relay_s, r.c_relay_r), 2 * i + k, near) for k, (src, dst) in enumerate(own_names)]
    def rope(acc, cos, sin, gain):
        scaled = unit_rms(acc) * gain
        low, high = scaled[:, :HEAD // 2], scaled[:, HEAD // 2:]
        return jnp.concatenate([low * cos - high * sin, high * cos + low * sin], axis=-1)

    def as_query(value):
        return (value.astype(BF16).astype(F32) * (HEAD ** -0.5)).astype(BF16)

    for i in range(N_CHUNK):
        x_copies[i].wait()

        def norm_rows(k, carry):
            these = aligned(i * chunk + k * 32, 32)
            part[these, :] = (unit_rms(xv[these, :].astype(F32)) * (1.0 + g_ref[0:1, :])).astype(BF16)
            return carry
        lax.fori_loop(0, chunk // 32, norm_rows, 0)
    for copy in t_copies:
        copy.wait()

    tall = 2 * chunk

    def local_tile(j, put):
        wait_w(0, j)

        def rows_step(c, carry):
            these = aligned(c * tall, tall)
            put(c, these, dot(part[these, :], wt[lax.rem(j, W_SLOTS)]))
            return carry
        lax.fori_loop(0, rows // tall, rows_step, 0)
        start_w(0, j + W_SLOTS)

    def v_step(j, carry):
        def put(c, these, acc):
            values[aligned(rows + c * tall, tall), cols(j)] = acc.astype(BF16)
        local_tile(j, put)
        return carry

    def k_step(j, carry):
        def put(c, these, acc):
            keys[aligned(rows + c * tall, tall), cols(j)] = rope(acc, cos_ref[these, :], sin_ref[these, :], 1.0 + qk_ref[1:2, :]).astype(BF16)
        local_tile(j + n_kv, put)
        return carry

    def q_step(j, carry):
        def put(c, these, acc):
            qo[these, cols(j)] = as_query(rope(acc, cos_ref[these, :], sin_ref[these, :], 1.0 + qk_ref[0:1, :]))
        local_tile(j + 2 * n_kv, put)
        return carry
    lax.fori_loop(0, n_kv, v_step, 0)
    lax.fori_loop(0, n_kv, k_step, 0)

    def window_sends(c):
        return [to_cp(buf.at[aligned(rows + row_start(c), chunk)], buf.at[chunk_rows(c)], (r.w_s, r.w_r), 2 * c + i, right) for i, buf in enumerate((keys, values))]

    entered(peers)

    @pl.when(jnp.logical_not(is_last))
    def _():
        for c in range(N_CHUNK):
            for copy in window_sends(c):
                copy.start()
    for copy in c_near:
        copy.start()

    def across_start(i, carry):
        for copy in c_across(i):
            copy.start()
        return carry
    lax.fori_loop(0, per_shard, across_start, 0)
    kv_out = [pltpu.make_async_copy(buf.at[pl.ds(rows, rows)], dst, r.kv_sem.at[i]) for i, (buf, dst) in enumerate(((keys, r.k_new_0), (values, r.v_new_0)))]
    for copy in kv_out:
        copy.start()
    lax.fori_loop(0, n_q, q_step, 0)
    start_wo(0)

    def to_tp(src, dst, send_sem, recv_sem, peer):
        return pltpu.make_async_remote_copy(src_ref=src, dst_ref=dst, send_sem=send_sem, recv_sem=recv_sem, device_id={'tp': peer}, device_id_type=MESH)

    def hop1(n):
        return to_tp(part.at[rows_of(n)], tot.at[rows_of(n)], r.s1.at[n], r.s1.at[n], mate)

    def hop2(n):
        return to_tp(part.at[rows_of(n)], recv2.at[lax.rem(n, RECV_SLOTS)], r.s2s.at[n], r.s2r.at[n], middle)

    def hop3(n):
        return to_tp(tot.at[rows_of(n)], tot.at[rows_of(n)], r.s3.at[n], r.s3.at[n], mate)

    def out_copy(n):
        return pltpu.make_async_copy(xv.at[rows_of(n)], r.x_out.at[rows_of(n)], r.out_sem.at[lax.rem(n, per)])

    def send_chunk(first):
        @pl.when(outer)
        def _():
            for i in range(N_SUB):
                hop1(first + i).start()

    def normalize(layer, n):
        start = sub_start(n)
        step = min(32, sub)
        kind = n // per

        def body(i, carry):
            these = aligned(start + i * step, step)
            value = (xv[these, :].astype(F32) + unit_rms(tot[these, :].astype(F32)) * (1.0 + g_ref[pl.ds(4 * layer + 1 + 2 * kind, 1), :])).astype(BF16)
            xv[these, :] = value
            part[these, :] = (unit_rms(value.astype(F32)) * (1.0 + g_ref[pl.ds(4 * layer + 2 + 2 * kind, 1), :])).astype(BF16)
            return carry
        lax.fori_loop(0, sub // step, body, 0)

        @pl.when((layer == 1) & (kind == 1))
        def _():
            out_copy(n).start()

    def event(clock):
        layer = clock // n_tick
        n = lax.rem(clock, n_tick)
        k, m = n - 1, n - LAG

        @pl.when(inner)
        def _():
            @pl.when(n < n_ev)
            def _():
                hop1(n).wait_recv()
                these = rows_of(n)
                part[these, :] = (part[these, :].astype(F32) + tot[these, :].astype(F32)).astype(BF16)

                @pl.when((n >= RECV_SLOTS) | (layer == 1))
                def _():
                    pl.semaphore_wait(r.credit, 1)
                hop2(n).start()

            @pl.when((k >= 0) & (k < n_ev))
            def _():
                hop2(k).wait_recv()
                hop2(k).wait_send()
                these = rows_of(k)
                tot[these, :] = (part[these, :].astype(F32) + recv2[lax.rem(k, RECV_SLOTS)].astype(F32)).astype(BF16)

                @pl.when((k < n_ev - RECV_SLOTS) | (layer == 0))
                def _():
                    pl.semaphore_signal(r.credit, inc=1, device_id={'tp': middle}, device_id_type=MESH)

            @pl.when((k >= 2) & (k <= n_ev))
            def _():
                hop3(k - 2).wait_send()

            @pl.when(k == n_ev)
            def _():
                hop3(n_ev - 1).wait_send()

        @pl.when(outer & (m >= 0))
        def _():
            hop1(m).wait_send()
            hop3(m).wait_recv()
        late = jnp.where(inner, k, m)

        @pl.when((late >= 0) & (late < n_ev))
        def _():
            normalize(layer, late)

            @pl.when(inner)
            def _():
                hop3(late).start()
        piece = n - 14

        @pl.when((layer == 0) & (piece >= 0) & (piece < per_shard * 2))
        def _():
            i = piece // 2

            @pl.when(lax.rem(piece, 2) == 0)
            def _():
                c_across(i)[0].wait_recv()
                c_relay(i)[0].start()

            @pl.when(lax.rem(piece, 2) == 1)
            def _():
                c_across(i)[1].wait_recv()
                c_relay(i)[1].start()

    def event_loop(low, high):
        def body(clock, carry):
            event(clock)
            return carry
        lax.fori_loop(low, high, body, 0)

    def project_chunk(layer, c):
        these = chunk_rows(c)

        def tile(t, carry):
            first = c * n_dim + t * O_TILES
            for i in range(O_TILES):
                wo_copy(layer, first + i).wait()
            for i in range(O_TILES):
                part[these, cols(t * O_TILES + i)] = dot(qo[these, :], wo_place(first + i)[0][...]).astype(BF16)
            for i in range(O_TILES):
                @pl.when(first + i + places < N_CHUNK * n_dim)
                def _():
                    wo_copy(layer, first + i + places).start()
            return carry
        lax.fori_loop(0, n_dim // O_TILES, tile, 0)
        send_chunk(c * N_SUB)

    @pl.when(is_first)
    def _():
        for copy in old_copies:
            copy.wait()
    span = rows + chunk

    def window_chunk(c, carry):
        @pl.when(jnp.logical_not(is_first))
        def _():
            for copy in window_sends(c):
                copy.wait_recv()
        these = chunk_rows(c)
        seen_keys = pl.ds(pl.multiple_of(row_start(c), chunk), span)
        row_id = lax.broadcasted_iota(jnp.int32, (chunk, span), 0)
        col_id = lax.broadcasted_iota(jnp.int32, (chunk, span), 1)
        seen = (col_id > row_id) & (col_id <= row_id + rows)
        def one_head(n, carry):
            kv = cols(n // groups)
            scores = jnp.where(seen, dot_t(qo[these, cols(n)], keys[seen_keys, kv]), NEG_BIG)
            best = jnp.max(scores, axis=-1, keepdims=True)
            prob = jnp.exp(scores - best)
            total = jnp.sum(prob, axis=-1, keepdims=True)
            qo[these, cols(n)] = (dot(prob.astype(BF16), values[seen_keys, kv]) / total).astype(BF16)
            return carry
        lax.fori_loop(0, n_q, one_head, 0)
        project_chunk(0, c)

        @pl.when(c > 0)
        def _():
            event(c - 1)
        return carry
    lax.fori_loop(0, N_CHUNK, window_chunk, 0)
    start_gu(0)

    @pl.when(jnp.logical_not(is_last))
    def _():
        for c in range(N_CHUNK):
            for copy in window_sends(c):
                copy.wait_send()
    for copy in kv_out:
        copy.wait()

    def feed_forward(layer, clock):
        marks = spread(N_SUB, [2] * n_ff + [1] * n_dim)

        def ffn_chunk(c, carry):
            these = chunk_rows(c)

            def task(t, carry):
                @pl.when(t < n_ff)
                def _():
                    i = c * n_ff + t
                    for copy in gu_copies(layer, i):
                        copy.wait()
                    slot = lax.rem(i, W_SLOTS // 2) * 2
                    lhs = part[these, :]
                    gate = dot(lhs, wt[slot])
                    up = dot(lhs, wt[slot + 1])
                    hact[:, cols(t)] = (jax.nn.gelu(gate, approximate=True) * up).astype(BF16)

                    @pl.when(i + W_SLOTS // 2 < N_CHUNK * n_ff)
                    def _():
                        for copy in gu_copies(layer, i + W_SLOTS // 2):
                            copy.start()

                @pl.when(t >= n_ff)
                def _():
                    i = c * n_dim + t - n_ff
                    dn_copy(layer, i).wait()
                    part[these, cols(t - n_ff)] = dot(hact[...], dn[lax.rem(i, D_SLOTS)]).astype(BF16)

                    @pl.when(i + D_SLOTS < N_CHUNK * n_dim)
                    def _():
                        dn_copy(layer, i + D_SLOTS).start()
                hit = t == marks[0]
                which = jnp.int32(0)
                for mark in marks[1:]:
                    which = which + (t >= mark).astype(jnp.int32)
                    hit = hit | (t == mark)

                @pl.when(hit)
                def _():
                    event(clock + c * N_SUB + which)
                return carry
            lax.fori_loop(0, n_ff + n_dim, task, 0)
            send_chunk(per + c * N_SUB)
            return carry
        lax.fori_loop(0, N_CHUNK, ffn_chunk, 0)
    lead = N_SUB + LAG
    event_loop(N_CHUNK - 1, lead)
    feed_forward(0, lead)
    start_dn(1)

    def turn_copies(c):
        return [pltpu.make_async_copy(table.at[chunk_rows(c)], r.turn.at[i], r.t_sem.at[i]) for i, table in enumerate((r.cos_global, r.sin_global))]

    def start_project(c):
        for copy in turn_copies(c):
            copy.start()
        for j in range(W_SLOTS):
            start_w(1, jnp.int32(j))
    start_project(0)

    new_names = ((r.k_all_1, r.k_new_1), (r.v_all_1, r.v_new_1))

    def new_sends(c):
        buf = lax.rem(c, 2)
        return [to_cp(r.fresh.at[buf, i], dst.at[cp, chunk_rows(c)], (r.n_s, r.n_r), c * 6 + 2 * k + i, peer) for k, peer in enumerate((across, far, near)) for i, (dst, _) in enumerate(new_names)]

    def new_local(c):
        buf = lax.rem(c, 2)
        return [pltpu.make_async_copy(r.fresh.at[buf, i], place, r.own_sem.at[buf, 2 * i + k]) for i, (every, mine) in enumerate(new_names) for k, place in enumerate((every.at[cp, chunk_rows(c)], mine.at[chunk_rows(c)]))]

    def free_fresh(c):
        for copy in new_sends(c):
            copy.wait_send()
        for copy in new_local(c):
            copy.wait()

    def global_project(c):
        these = chunk_rows(c)
        buf = lax.rem(c, 2)
        @pl.when(c >= 2)
        def _():
            free_fresh(c - 2)
        for copy in turn_copies(c):
            copy.wait()

        def tile(j):
            wait_w(1, j)
            return dot(part[these, :], wt[lax.rem(j, W_SLOTS)])

        def gv_step(j, carry):
            r.fresh[buf, 1, :, cols(j)] = tile(j).astype(BF16)
            start_w(1, j + W_SLOTS)
            return carry

        def gk_step(j, carry):
            r.fresh[buf, 0, :, cols(j)] = rope(tile(j + n_kv), r.turn[0], r.turn[1], 1.0 + qk_ref[3:4, :]).astype(BF16)
            start_w(1, j + n_kv + W_SLOTS)
            return carry

        def gq_step(j, carry):
            qo[these, cols(j)] = as_query(rope(tile(j + 2 * n_kv), r.turn[0], r.turn[1], 1.0 + qk_ref[2:3, :]))
            start_w(1, j + 2 * n_kv + W_SLOTS)
            return carry
        lax.fori_loop(0, n_kv, gv_step, 0)
        lax.fori_loop(0, n_kv, gk_step, 0)
        for copy in new_sends(c) + new_local(c):
            copy.start()
        lax.fori_loop(0, n_q, gq_step, 0)

        @pl.when(c + 1 < N_CHUNK)
        def _():
            start_project(c + 1)

    n_pass = 2 * per_shard
    n_mask = -(-(shard // 2) // block)
    first_pos = r.first_pos[0]
    stack = groups * chunk
    step = min(256, stack)
    scores_refs = (r.s_even, r.s_odd)
    pair = cp // 2

    def pass_size(p):
        return jnp.where(p == 2, cp + 1, n_pass)

    def shard_of(p, b):
        return 2 * lax.rem(pair + p, 2) + lax.rem(b // per_shard, 2)

    def fetch(p, b, own, every, new, dst, sem, op):
        s = shard_of(p, b)
        where = aligned(lax.rem(b, per_shard) * block, block)

        @pl.when((p < 2) & (s == cp))
        def _():
            op(pltpu.make_async_copy(own.at[where], dst, sem))

        @pl.when((p < 2) & (s != cp))
        def _():
            op(pltpu.make_async_copy(every.at[s, where], dst, sem))

        @pl.when(p == 2)
        def _():
            op(pltpu.make_async_copy(new.at[lax.rem(b, size)], dst, sem))

    def fetch_k(p, b, op):
        slot = lax.rem(b, 3)
        fetch(p, b, r.k_own, r.k_all, r.k_all_1, keys.at[aligned(slot * block, block)], r.kb_sem.at[slot], op)

    def fetch_v(p, b, op):
        slot = lax.rem(b, 2)
        fetch(p, b, r.v_own, r.v_all, r.v_all_1, values.at[aligned(slot * block, block)], r.vb_sem.at[slot], op)

    def begin_pass(p):
        fetch_k(p, 0, begin)
        fetch_v(p, 0, begin)

        @pl.when(pass_size(p) > 1)
        def _():
            fetch_k(p, 1, begin)

    def raw_scores(c, head, slot):
        query = jnp.concatenate([qo[chunk_rows(c), (head * groups + g) * HEAD:(head * groups + g + 1) * HEAD] for g in range(groups)], axis=0)
        scores_refs[head][...] = dot_t(query, keys[aligned(slot * block, block), head * HEAD:(head + 1) * HEAD])

    def state(c, head, low, length):
        return aligned(lax.rem(c, 2) * half + head * stack + low, length)

    def absorb(c, head, slot, bound):
        value = values[aligned(slot * block, block), head * HEAD:(head + 1) * HEAD]
        for low in range(0, stack, step):
            scores = scores_refs[head][low:low + step, :]
            if bound is not None:
                limit, by_row = bound
                row_id = lax.rem(low, chunk) + lax.rem(lax.broadcasted_iota(jnp.int32, scores.shape, 0), chunk)
                scores = jnp.where(lax.broadcasted_iota(jnp.int32, scores.shape, 1) < limit + by_row * row_id, scores, NEG_BIG)
            these = state(c, head, low, step)
            old = top[these, :]
            new = jnp.maximum(old, jnp.max(scores, axis=-1, keepdims=True))
            decay = jnp.exp(old - new)
            prob = jnp.exp(scores - jnp.concatenate([new] * (block // 128), axis=1))
            lanes = prob[:, :128]
            for i in range(1, block // 128):
                lanes = lanes + prob[:, i * 128:(i + 1) * 128]
            sums[these, :] = sums[these, :] * decay + lanes
            top[these, :] = new
            acc_ref[these, :] = acc_ref[these, :] * jnp.concatenate([decay] * (HEAD // 128), axis=1) + dot(prob.astype(BF16), value)

    def job_step(j, carry):
        second = j // 6
        c = (1 - second) * lax.rem(j, 2) + second * (j // 3)
        p = (1 - second) * (j // 2) + second * lax.rem(j, 3)

        @pl.when((j < 2) | (j == 3))
        def _():
            low = j - j // 3

            def body(i, carry):
                before = lead + 16 + 3 * i + 2 * (i // 2) - 2 * (i // 3)
                event_loop(before, before + 1 + 2 * (i // 3))
                global_project(i)
                return carry
            lax.fori_loop(low, low + 1 + j // 3, body, 0)

            @pl.when(j == 3)
            def _():
                start_wo(1)

        @pl.when(p == 0)
        def _():
            for ref, value in ((top, NEG_BIG), (sums, 0.0), (acc_ref, 0.0)):
                ref[state(c, 0, 0, half), :] = jnp.full((half, ref.shape[1]), value, F32)
        count = pass_size(p)
        n_free = jnp.where(p == 2, cp, n_pass - n_mask)
        base = jnp.where(second == 1, n_tick + 1 + 5 * ((j - 6) // 3) + 2 * lax.rem(j, 3), jnp.where(j == 5, n_tick, lead + 17 + 3 * j - j // 2))
        fetch_k(p, 0, end)
        raw_scores(c, 0, 0)

        def block_step(masked, b, carry):
            fetch_v(p, b, end)

            @pl.when(b + 1 < count)
            def _():
                fetch_k(p, b + 1, end)
                fetch_v(p, b + 1, begin)

            @pl.when(b + 2 < count)
            def _():
                fetch_k(p, b + 2, begin)
            bound = None
            if masked:
                limit = jnp.where(p == 2, row_start(c) + 1, jnp.where(shard_of(p, b) == size - 1, first_pos - (size - 1) * shard - lax.rem(b, per_shard) * block, block))
                bound = (limit, jnp.where(p == 2, 1, 0))
            slot, later, v_slot = lax.rem(b, 3), lax.rem(b + 1, 3), lax.rem(b, 2)
            raw_scores(c, 1, slot)
            absorb(c, 0, v_slot, bound)
            raw_scores(c, 0, later)
            absorb(c, 1, v_slot, bound)
            if not masked:
                @pl.when((b == (n_pass - n_mask) // 2) & (p < 2) & (j != 3))
                def _():
                    event(base)
            return carry
        lax.fori_loop(0, n_free, functools.partial(block_step, False), 0)
        lax.fori_loop(n_free, count, functools.partial(block_step, True), 0)

        @pl.when(j == 1)
        def _():
            def body(i, carry):
                for copy in c_relay(i):
                    copy.wait_recv()
                return carry
            lax.fori_loop(0, per_shard, body, 0)

        @pl.when(j == 3)
        def _():
            free_fresh(2)
            free_fresh(3)

            def body(i, carry):
                for copy in new_sends(i):
                    copy.wait_recv()
                return carry
            lax.fori_loop(0, N_CHUNK, body, 0)

        @pl.when(j < 11)
        def _():
            after = j + 1
            begin_pass((1 - after // 6) * (after // 2) + (after // 6) * lax.rem(after, 3))

        @pl.when(p == 2)
        def _():
            these = chunk_rows(c)
            for head in range(n_kv):
                whole = state(c, head, 0, stack)
                total = jnp.sum(sums[whole, :], axis=-1, keepdims=True)
                result = (acc_ref[whole, :] / total).astype(BF16)
                for g in range(groups):
                    qo[these, (head * groups + g) * HEAD:(head * groups + g + 1) * HEAD] = result[g * chunk:(g + 1) * chunk]
            project_chunk(1, c)

        @pl.when((j != 3) & (j != 4))
        def _():
            event(base + jnp.where(p < 2, 1, 0))
        return carry
    for copy in c_near:
        copy.wait()
    begin_pass(jnp.int32(0))
    lax.fori_loop(0, 12, job_step, 0)
    start_gu(1)
    clock = n_tick + 11
    feed_forward(1, clock)
    event_loop(clock + N_CHUNK * N_SUB, 2 * n_tick)

    def finish(m, carry):
        out_copy(m).wait()
        return carry
    lax.fori_loop(0, per, finish, 0)

    def gathered(i, carry):
        for copy in c_across(i) + c_relay(i):
            copy.wait_send()
        return carry
    lax.fori_loop(0, per_shard, gathered, 0)


def run_layers(ins, collective_id):
    rows, dim = ins['x'].shape
    q_cols, kv_cols, ff = ins['w_query'].shape[2], ins['w_key'].shape[2], ins['w_gate'].shape[2]
    shard = ins['k_own'].shape[0]
    chunk = rows // N_CHUNK
    sub = chunk // N_SUB
    n_ev = 2 * N_CHUNK * N_SUB
    groups, n_kv = q_cols // kv_cols, kv_cols // HEAD
    stack = groups * chunk
    pieces = 2 * (shard // rows)

    def spec(name):
        if name == 'first_pos':
            return pl.BlockSpec(memory_space=pltpu.SMEM)
        return pl.BlockSpec(memory_space=pltpu.VMEM if name in ('gains', 'qk_gains') else pl.ANY)
    array = jax.ShapeDtypeStruct
    made = array((rows, kv_cols), BF16)
    outs = dict(x_out=array((rows, dim), BF16), k_new_0=made, v_new_0=made, k_new_1=made, v_new_1=made)
    outs |= dict(k_all=array((4, shard, kv_cols), BF16), v_all=array((4, shard, kv_cols), BF16), k_all_1=array((4, rows, kv_cols), BF16), v_all_1=array((4, rows, kv_cols), BF16))
    dma = pltpu.SemaphoreType.DMA
    scratch = dict(
        part=pltpu.VMEM((rows, dim), BF16),
        tot=pltpu.VMEM((rows, dim), BF16),
        xv=pltpu.VMEM((rows, dim), BF16),
        wt=pltpu.VMEM((W_SLOTS, dim, TILE), BF16),
        dn=pltpu.VMEM((D_SLOTS, ff, TILE), BF16),
        qo=pltpu.VMEM((rows, q_cols), BF16),
        hact=pltpu.VMEM((chunk, ff), BF16),
        recv2=pltpu.VMEM((RECV_SLOTS, sub, dim), BF16),
        keys=pltpu.VMEM((3 * rows, kv_cols), BF16),
        values=pltpu.VMEM((2 * rows, kv_cols), BF16),
        fresh=pltpu.VMEM((2, 2, chunk, kv_cols), BF16),
        turn=pltpu.VMEM((2, chunk, HEAD // 2), F32),
        s_even=pltpu.VMEM((stack, rows), F32),
        s_odd=pltpu.VMEM((stack, rows), F32),
        top=pltpu.VMEM((2 * n_kv * stack, 128), F32),
        sums=pltpu.VMEM((2 * n_kv * stack, 128), F32),
        acc=pltpu.VMEM((2 * n_kv * stack, HEAD), F32),
        w_sem=dma((W_SLOTS,)), wo_sem=dma((W_SLOTS * (dim // q_cols),)), dn_sem=dma((D_SLOTS,)), x_sem=dma((N_CHUNK,)), t_sem=dma((2,)), old_sem=dma((2,)),
        kv_sem=dma((2,)), own_sem=dma((2, 4)), kb_sem=dma((3,)), vb_sem=dma((2,)), out_sem=dma((n_ev // 2,)),
        w_s=dma((2 * N_CHUNK,)), w_r=dma((2 * N_CHUNK,)), n_s=dma((6 * N_CHUNK,)), n_r=dma((6 * N_CHUNK,)),
        c_near_s=dma((2,)), c_near_r=dma((2,)), c_across_s=dma((pieces,)), c_across_r=dma((pieces,)), c_relay_s=dma((pieces,)), c_relay_r=dma((pieces,)),
        s1=dma((n_ev,)), s2s=dma((n_ev,)), s2r=dma((n_ev,)), s3=dma((n_ev,)),
        credit=pltpu.SemaphoreType.REGULAR,
    )
    names = tuple(ins) + tuple(outs) + tuple(scratch)
    made = pl.pallas_call(
        functools.partial(layers_kernel, names),
        out_shape=tuple(outs.values()),
        in_specs=[spec(name) for name in ins],
        out_specs=tuple(pl.BlockSpec(memory_space=pl.ANY) for _ in outs),
        scratch_shapes=list(scratch.values()),
        compiler_params=pltpu.CompilerParams(collective_id=collective_id, has_side_effects=True, vmem_limit_bytes=VMEM_LIMIT),
        name='two_layers',
    )(*ins.values())
    return dict(zip(outs, made))


def solution(mesh):
    row_spec = P(('dp', 'cp'), None)
    cache_spec = P(('dp', 'cp'), 'tp', None)
    window_spec = P('dp', 'tp', None)
    col_spec = P(None, None, 'tp')
    row_split = P(None, 'tp', None)
    replicated = P()

    def device_step(hidden, start_pos, k_local, v_local, k_global, v_global, w_query, w_key, w_value, w_out, w_gate, w_up, w_down, norm_gain, qk_gain):
        first_pos = start_pos[0]
        cp_index = lax.axis_index('cp')
        rows, dim = hidden.shape
        window = k_local.shape[0]
        flat = lambda a: a.reshape(a.shape[0], -1)
        gains = jnp.concatenate([norm_gain.reshape(8, dim), jnp.zeros((8, dim), F32)], axis=0)
        qk_gains = jnp.concatenate([qk_gain.reshape(4, HEAD), jnp.zeros((4, HEAD), F32)], axis=0)
        turn = jnp.remainder(first_pos, window)
        rolled = [flat(lax.dynamic_slice_in_dim(jnp.concatenate([a, a], axis=0), turn, window, axis=0)) for a in (k_local, v_local)]
        cos_local, sin_local = rope_tables(first_pos + cp_index * rows, rows, LOCAL_BASE, 1.0)
        cos_global, sin_global = rope_tables(first_pos + cp_index * rows, rows, GLOBAL_BASE, GLOBAL_DIV)
        made = run_layers(dict(
            first_pos=start_pos, x=hidden, gains=gains, qk_gains=qk_gains,
            cos_local=cos_local, sin_local=sin_local, cos_global=cos_global, sin_global=sin_global,
            w_query=w_query, w_key=w_key, w_value=w_value, w_out=w_out, w_gate=w_gate, w_up=w_up, w_down=w_down,
            k_old=rolled[0], v_old=rolled[1], k_own=flat(k_global), v_own=flat(v_global),
        ), 0)
        shaped = lambda a: a.reshape(rows, -1, HEAD)
        return made['x_out'], shaped(made['k_new_0']), shaped(made['v_new_0']), shaped(made['k_new_1']), shaped(made['v_new_1'])

    return jax.shard_map(device_step, mesh=mesh, in_specs=(row_spec, P('dp'), window_spec, window_spec, cache_spec, cache_spec, col_spec, col_spec, col_spec, row_split, col_spec, col_spec, row_split, replicated, replicated), out_specs=(row_spec, cache_spec, cache_spec, cache_spec, cache_spec), check_vma=False)
```

time: 2430 us -> 909 us (0.37)
  waiting for transfers between devices: 1270 us -> 0 us
  Pallas kernels: 0 us -> 868 us
  matrix products: 767 us -> 0 us
  other arithmetic: 260 us -> 9.89 us
  local copies, waits for them, and re-layouts: 88 us -> 28.6 us
    psum x4 -> x0, waiting for transfers between devices: 1070 us -> none  [the longest x2 549 us: finish(): lax.psum(jnp.dot(attn_out.reshape(row_count, -1), w_out, preferred_elemen...]
    pallas_call x0 -> x1, Pallas kernels: none -> 868 us  [run_layers(): pl.pallas_call(functools.partial(layers_kernel, names), out_shape=tuple(o...]
    dot_general x31 -> x0, matrix products: 740 us -> none  [the longest x4 155 us: partial_block(): jnp.einsum('qkgt,tkd->qkgd', cache_exp.astype(jnp.bfloat16), cache_v, pre...]
    reduce_sum x18 -> x0, other arithmetic: 210 us -> none  [the longest x8 156 us: partial_block(): row_sum = cache_exp.sum(axis=-1) + own_exp.sum(axis=-1)]
    all_to_all x1 -> x0, waiting for transfers between devices: 181 us -> none  [spread_attention(): got_out = lax.all_to_all(part_out, 'cp', 0, 0, tiled=True)]
    dot_general x6 -> x0, local copies, waits for them, and re-layouts: 43.5 us -> none  [the longest x3 27.2 us: project(): jnp.dot(normed, w_query, preferred_element_type=jnp.float32)]
    sub x1 -> x0, matrix products: 27.8 us -> none  [window_attention(): attn_prob = jax.nn.softmax(scores, axis=-1).astype(jnp.bfloat16)]
  transfers between devices with their start and end apart: 8 -> 0, of which waited for: 6 -> 0; matrix products, arithmetic and copies ran while one was open for 6% -> 0% of each run, Pallas kernels for 0% -> 0%
where the time goes in v3:
time: 909 us; the launch traced here: 908 us
  Pallas kernels  868 us (95%)
  local copies, waits for them, and re-layouts  28.6 us (3%)
  other arithmetic  9.89 us (1%)
    pallas_call x1, Pallas kernels, run_layers(): pl.pallas_call(functools.partial(layers_kernel, names), out_shape=tuple(o...  868 us

profile of v3, /device:TPU:4, one launch (start us, length us, event | category | flops | bytes accessed | tf_op | source)
XLA Modules:
  0.0 908.3 jit_solution(14684661237235444466)
XLA Ops:
  0.6 0.0 slice-start
  1.5 0.7 reshape.438
  2.2 0.6 concatenate.13.refs_3_
  2.8 0.1 multiply_sine_fusion.3
  3.0 0.1 multiply_sine_fusion.2
  3.1 0.1 multiply_sine_fusion.1
  3.3 0.1 multiply_sine_fusion
  3.4 0.9 reshape.437
  4.4 0.7 concatenate.12.refs_2_
  5.1 1.1 multiply_add_fusion
  6.2 1.1 multiply_add_fusion.1
  7.3 0.0 slice-start.1
  7.3 7.1 fusion
  14.4 1.2 copy.21
  15.6 0.0 slice-start.2
  15.6 1.2 copy.20
  16.8 0.0 slice-done
  16.8 0.0 slice-done.1
  16.8 0.0 slice-start.3
  16.8 3.8 copy.22
  20.7 0.0 slice-done.2
  20.7 0.0 slice-done.3
  20.7 3.8 copy.23
  24.5 868.3 %two_layers.1 = (bf16[1024,3840]{1,0:T(8,128)(2,1)}, bf16[1024,512]{1,0:T(8,128)(2,1)}, bf16[1024,512]{1,0:T(8,128)(2,1)}, bf16[1024,512]{1,0:T(8,128)(2,1)}, bf...) custom-call(s32[1]{0:T(128)} %copy.25.refs_0_, ...), custom_call_target="tpu_custom_call" | custom-call | tf_op jit(solution)/shard_map/two_layers/pallas_call | solution.py:807
  892.8 2.1 reshape.443
  894.9 2.1 reshape.444
  897.0 2.1 reshape.445
  899.2 2.1 reshape.446
  901.3 7.0 copy.26
  (8 shorter events, 0.0 us)
Async XLA Ops:
  0.6 16.2 %slice-start = ((s8[6291456]{0:T(1024)(128)(4,1)}), s8[2097152]{0:T(1024)(128)(4,1)S(1)}, s32[]{:S(2)}) async-start(s8[6291456]{0:T(1024)(128)(4,1)} %bitcast.27), calls=%async_computation | async-start | bytes 4194304
  7.3 9.5 %slice-start.1 = ((s8[6291456]{0:T(1024)(128)(4,1)}), s8[4194304]{0:T(1024)(128)(4,1)S(1)}, s32[]{:S(2)}) async-start(s8[6291456]{0:T(1024)(128)(4,1)} %bitcast.27), calls=%async_computation.1 | async-start | bytes 8388608
  15.6 5.1 slice-start.2
  16.8 3.8 slice-start.3
